TPU v7x, 512 devices: a whole 4x8x8 slice. The times are simulated.
512 devices in a mesh: gx: 8 (over y_lo, x), gy: 8 (over z), gz: 8 (over y_hi, core).
Axes of the slice: x: 4, y: 8 (y_hi: 4, y_lo: 2; y = y_hi * 2 + y_lo), z: 8, core: 2. Of those that a mesh axis runs over, the one named last changes fastest.
Arguments:
- material: int32 [256, 512, 1024], P('gx', 'gy', 'gz'), may hold values from 0 to 7
- eps_table: float32 [8], replicated, may hold values from 1 to 13
- grading: bfloat16 [256, 512, 1024], P('gx', 'gy', 'gz'), may hold values from 0.25 to 1.75
Outputs:
- smoothed: bfloat16 [6, 256, 512, 1024], P(None, 'gx', 'gy', 'gz')
All inputs are finite; a program needn't handle non-finite values.
Results may differ from a plain program's by a relative error of at most 0.001.
Values sent between devices are 32-bit elements; how exact they have to be, the bound alone decides.
No kernel may reach another device: no remote copies, remote signals or barrier semaphores. Data moves between devices by JAX's collectives and lax.ppermute only.
A program may use at most 64 MiB of HBM per device.

v0:
```python
import jax
import jax.numpy as jnp
from jax import lax
from jax.sharding import PartitionSpec as P


def padded_2(block, sides, width):
    for axis, dim in sides:
        count = lax.axis_size(axis)
        forward = [(i, i + 1) for i in range(count - 1)]
        forward.append((count - 1, 0))
        backward = [(target, source) for source, target in forward]
        low = lax.ppermute(
            lax.slice_in_dim(block, block.shape[dim] - width, None, axis=dim), axis, forward
        )
        high = lax.ppermute(lax.slice_in_dim(block, 0, width, axis=dim), axis, backward)
        block = jnp.concatenate([low, block, high], axis=dim)
    return block


def lookup(material, eps_table, grading):
    values = jnp.zeros(material.shape, jnp.float32)
    for index in range(eps_table.shape[0]):
        values = jnp.where(material == index, eps_table[index], values)
    return values * grading.astype(jnp.float32)


def box_mean(padded):
    total = padded[:-2] + padded[1:-1] + padded[2:]
    total = total[:, :-2] + total[:, 1:-1] + total[:, 2:]
    total = total[:, :, :-2] + total[:, :, 1:-1] + total[:, :, 2:]
    return total / 27.0


def tensor(mean_ext, mean_inv):
    centre = mean_ext[1:-1, 1:-1, 1:-1]
    grad_x = (mean_ext[2:, 1:-1, 1:-1] - mean_ext[:-2, 1:-1, 1:-1]) * 0.5
    grad_y = (mean_ext[1:-1, 2:, 1:-1] - mean_ext[1:-1, :-2, 1:-1]) * 0.5
    grad_z = (mean_ext[1:-1, 1:-1, 2:] - mean_ext[1:-1, 1:-1, :-2]) * 0.5
    scale = 1.0 / (grad_x * grad_x + grad_y * grad_y + grad_z * grad_z + 0.1)
    recip = 1.0 / centre
    grads = (grad_x, grad_y, grad_z)
    pairs = ((0, 0), (1, 1), (2, 2), (0, 1), (0, 2), (1, 2))
    result = []
    for first, second in pairs:
        weight = grads[first] * grads[second] * scale
        delta = 1.0 if first == second else 0.0
        result.append(mean_inv * weight + (delta - weight) * recip)
    return jnp.stack(result, 0).astype(jnp.bfloat16)


def local(material, eps_table, grading):
    eps = lookup(material, eps_table, grading)
    padded = padded_2(eps, (("gx", 0), ("gy", 1), ("gz", 2)), 2)
    mean_ext = box_mean(padded)
    mean_inv = box_mean(1.0 / padded[1:-1, 1:-1, 1:-1])
    return tensor(mean_ext, mean_inv)


def solution(mesh):
    return jax.shard_map(
        local,
        mesh=mesh,
        in_specs=(P("gx", "gy", "gz"), P(), P("gx", "gy", "gz")),
        out_specs=P(None, "gx", "gy", "gz"),
        check_vma=False,
    )
```

profile of v0, /device:TPU:23, one launch (start us, length us, event | category | flops | bytes accessed | tf_op | source)
XLA Modules:
  0.0 73.3 jit_solution(4026944462059677747)
XLA Ops:
  0.0 1.6 %fusion.23 = (f32[1]{0:T(128)}, f32[1]{0:T(128)}, f32[1]{0:T(128)}, f32[1]{0:T(128)}, f32[1]{0:T(128)}, /*index=5*/f32[1]{0:T(128)}, f32[1]{0:T(128)}, f32[1]{0:T(128)}) fusion(f32[8]{0:T(128)} %param.4), kind=kLoop, calls=%fused_computation.49 | loop fusion | bytes 64 | tf_op jit(solution)/shard_map/slice | solution.py:24
  1.6 7.0 %convert_multiply_fusion = f32[32,64,128]{2,1,0:T(8,128)S(1)} fusion(bf16[32,64,128]{2,1,0:T(8,128)(2,1)} %param.5, s32[32,64,128]{2,1,0:T(8,128)} %param.3, f32[]{:T(128)} %bitcast.7, f32[]{:T(128)} %bitcast.6, f32[]{:T(128)} %bitcast.5, f32[]{:T(128)} %bitcast.4, f32[]{:T(128)} %bitcast.3, f32[]{:T(128)} %bitcast.2, f32[]{:T(128)} %bitcast.1, f32[]{:T(128)} %bitcast), kind=kLoop, calls=%fused_computation.31 | loop fusion | flops 4718592 | bytes 2621472 | tf_op jit(solution)/shard_map/mul | solution.py:25
  8.6 3.1 %collective-permute-start = (f32[2,64,128]{2,1,0:T(8,128)S(1)}, f32[2,64,128]{2,1,0:T(8,128)S(1)}, u32[]{:S(2)}, u32[]{:S(2)}) collective-permute-start(f32[2,64,128]{2,1,0:T(8,128)S(1)} %get-tuple-element.14), channel_id=1, source_target_pairs={{0,64},{64,128},{128,192},{192,256},{256,320},{320,384},{384,448},... | collective-permute-start | bytes 196616 | tf_op jit(solution)/shard_map/ppermute | solution.py:13
  11.7 2.2 %collective-permute-start.1 = (f32[2,64,128]{2,1,0:T(8,128)S(1)}, f32[2,64,128]{2,1,0:T(8,128)S(1)}, u32[]{:S(2)}, u32[]{:S(2)}) collective-permute-start(f32[2,64,128]{2,1,0:T(8,128)S(1)} %get-tuple-element.15), channel_id=1, source_target_pairs={{64,0},{128,64},{192,128},{256,192},{320,256},{384,320},{448,384},... | collective-permute-start | bytes 196616 | tf_op jit(solution)/shard_map/ppermute | solution.py:16
  13.9 0.0 collective-permute-done
  13.9 4.9 %collective-permute-done.1 = f32[2,64,128]{2,1,0:T(8,128)S(1)} collective-permute-done((f32[2,64,128]{2,1,0:T(8,128)S(1)}, f32[2,64,128]{2,1,0:T(8,128)S(1)}, u32[]{:S(2)}, u32[]{:S(2)}) %collective-permute-start.1) | collective-permute-done | bytes 65568 | tf_op jit(solution)/shard_map/ppermute | solution.py:16
  18.9 4.0 %collective-permute-start.2 = (f32[36,2,128]{2,1,0:T(2,128)S(1)}, f32[36,2,128]{2,1,0:T(2,128)S(1)}, u32[]{:S(2)}, u32[]{:S(2)}) collective-permute-start(f32[36,2,128]{2,1,0:T(2,128)S(1)} %get-tuple-element.12), channel_id=1, source_target_pairs={{0,8},{8,16},{16,24},{24,32},{32,40},{40,48},{48,56},{56,0},{1,9},... | collective-permute-start | bytes 110600 | tf_op jit(solution)/shard_map/ppermute | solution.py:13
  22.9 8.6 %collective-permute-start.3 = (f32[36,2,128]{2,1,0:T(2,128)S(1)}, f32[36,2,128]{2,1,0:T(2,128)S(1)}, u32[]{:S(2)}, u32[]{:S(2)}) collective-permute-start(f32[36,2,128]{2,1,0:T(2,128)S(1)} %get-tuple-element.13), channel_id=1, source_target_pairs={{8,0},{16,8},{24,16},{32,24},{40,32},{48,40},{56,48},{0,56},{9,1},... | collective-permute-start | bytes 110600 | tf_op jit(solution)/shard_map/ppermute | solution.py:16
  31.5 0.0 collective-permute-done.2
  31.5 1.0 %collective-permute-done.3 = f32[36,2,128]{2,1,0:T(2,128)S(1)} collective-permute-done((f32[36,2,128]{2,1,0:T(2,128)S(1)}, f32[36,2,128]{2,1,0:T(2,128)S(1)}, u32[]{:S(2)}, u32[]{:S(2)}) %collective-permute-start.3) | collective-permute-done | bytes 36896 | tf_op jit(solution)/shard_map/ppermute | solution.py:16
  32.5 0.1 pad_maximum_fusion.1
  32.7 1.5 %fusion.21 = (f32[36,68,2]{2,1,0:T(8,128)}, f32[36,68,2]{2,1,0:T(8,128)S(1)}) fusion(f32[36,68,128]{2,1,0:T(8,128)S(1)} %pad_maximum_fusion.1), kind=kLoop, calls=%fused_computation.47 | loop fusion | bytes 78336 | tf_op jit(solution)/shard_map/slice | solution.py:14
  34.2 1.8 %copy.14 = f32[36,68,2]{1,2,0:T(2,128)S(1)} copy(f32[36,68,2]{2,1,0:T(8,128)} %get-tuple-element.10) | data formatting | bytes 39168 | tf_op jit(solution)/shard_map/slice | solution.py:14
  36.0 7.4 %collective-permute-start.4 = (f32[36,68,2]{1,2,0:T(2,128)S(1)}, f32[36,68,2]{1,2,0:T(2,128)S(1)}, u32[]{:S(2)}, u32[]{:S(2)}) collective-permute-start(f32[36,68,2]{1,2,0:T(2,128)S(1)} %copy.14), channel_id=1, source_target_pairs={{0,1},{1,2},{2,3},{3,4},{4,5},{5,6},{6,7},{7,0},{8,9},{9,10},{10,1... | collective-permute-start | bytes 58760 | tf_op jit(solution)/shard_map/ppermute | solution.py:13
  43.4 0.5 copy.15
  43.8 1.9 %collective-permute-start.5 = (f32[36,68,2]{1,2,0:T(2,128)S(1)}, f32[36,68,2]{1,2,0:T(2,128)S(1)}, u32[]{:S(2)}, u32[]{:S(2)}) collective-permute-start(f32[36,68,2]{1,2,0:T(2,128)S(1)} %copy.15), channel_id=1, source_target_pairs={{1,0},{2,1},{3,2},{4,3},{5,4},{6,5},{7,6},{0,7},{9,8},{10,9},{11,1... | collective-permute-start | bytes 58760 | tf_op jit(solution)/shard_map/ppermute | solution.py:16
  45.8 0.0 collective-permute-done.4
  45.8 0.6 copy.16
  46.4 4.9 %collective-permute-done.5 = f32[36,68,2]{1,2,0:T(2,128)S(1)} collective-permute-done((f32[36,68,2]{1,2,0:T(2,128)S(1)}, f32[36,68,2]{1,2,0:T(2,128)S(1)}, u32[]{:S(2)}, u32[]{:S(2)}) %collective-permute-start.5) | collective-permute-done | bytes 19616 | tf_op jit(solution)/shard_map/ppermute | solution.py:16
  51.2 1.6 %copy.17 = f32[36,68,2]{2,1,0:T(8,128)} copy(f32[36,68,2]{1,2,0:T(2,128)S(1)} %collective-permute-done.5) | data formatting | bytes 39168 | tf_op jit(solution)/shard_map/ppermute | solution.py:16
  52.8 2.6 %pad_maximum_fusion = f32[36,68,132]{2,1,0:T(8,128)S(1)} fusion(f32[36,68,2]{2,1,0:T(8,128)} %copy.17, f32[36,2,128]{2,1,0:T(2,128)S(1)} %collective-permute-done.3, f32[2,64,128]{2,1,0:T(8,128)S(1)} %collective-permute-done.1, f32[32,64,128]{2,1,0:T(8,128)S(1)} %convert_multiply_fusion, f32[2,64,128]{2,1,0:T(8,128)S(1)} %collective-permute-done, ...), kind=kLoop, calls=%fused_computation | loop fusion | flops 1938816 | bytes 2585088 | tf_op jit(solution)/shard_map/concatenate | solution.py:17
  55.4 0.2 slice_add_fusion.4
  55.6 0.8 %slice_divide_fusion = f32[34,66,130]{2,1,0:T(8,128)S(1)} fusion(f32[36,68,132]{2,1,0:T(8,128)S(1)} %pad_maximum_fusion), kind=kLoop, calls=%fused_computation.8 | loop fusion | flops 291720 | bytes 2333760 | tf_op jit(solution)/shard_map/div | solution.py:56
  56.4 0.2 slice_add_fusion.6
  56.6 1.7 %slice_add_fusion.8 = f32[32,64,130]{2,1,0:T(8,128)} fusion(f32[32,66,130]{2,1,0:T(8,128)S(1)} %slice_add_fusion.6), kind=kLoop, calls=%fused_computation.11 | loop fusion | flops 532480 | bytes 4259840 | tf_op jit(solution)/shard_map/add | solution.py:30
  58.4 0.5 slice_add_fusion.2
  58.8 1.4 %fusion = f32[34,66,130]{2,1,0:T(8,128)S(1)} fusion(f32[34,66,132]{2,1,0:T(8,128)S(1)} %slice_add_fusion.2), kind=kLoop, calls=%fused_computation.2 | loop fusion | flops 875160 | bytes 4667520 | tf_op jit(solution)/shard_map/div | solution.py:32
  60.2 5.6 %fusion.6 = (bf16[6,32,64,128]{3,2,1,0:T(8,128)(2,1)}, f32[32,64,128]{2,1,0:T(8,128)S(1)}, f32[32,64,128]{2,1,0:T(8,128)S(1)}, f32[32,64,128]{2,1,0:T(8,128)S(1)}, f32[32,64,128]{2,1,0:T(8,128)S(1)}) fusion(f32[34,66,130]{2,1,0:T(8,128)S(1)} %fusion, f32[32,64,130]{2,1,0:T(8,128)} %slice_add_fusion.8), kind=kLoop, calls=%fused_computation.33 | loop fusion | flops 6029311 | bytes 15204352
  65.8 1.5 %fusion.8 = bf16[6,32,64,128]{3,2,1,0:T(8,128)(2,1)} fusion(bf16[6,32,64,128]{3,2,1,0:T(8,128)(2,1)} %get-tuple-element.5, f32[32,64,128]{2,1,0:T(8,128)S(1)} %get-tuple-element.9, f32[32,64,128]{2,1,0:T(8,128)S(1)} %get-tuple-element.6, f32[34,66,130]{2,1,0:T(8,128)S(1)} %fusion, f32[32,64,128]{2,1,0:T(8,128)S(1)} %get-tuple-element.7, ...), kind=kLoop, calls=%fused_computation.35 | loop fusion | flops 3670016 | bytes 5767168
  67.3 1.5 %fusion.10 = bf16[6,32,64,128]{3,2,1,0:T(8,128)(2,1)} fusion(bf16[6,32,64,128]{3,2,1,0:T(8,128)(2,1)} %fusion.8, f32[32,64,128]{2,1,0:T(8,128)S(1)} %get-tuple-element.9, f32[32,64,128]{2,1,0:T(8,128)S(1)} %get-tuple-element.7, f32[34,66,130]{2,1,0:T(8,128)S(1)} %fusion, f32[32,64,128]{2,1,0:T(8,128)S(1)} %get-tuple-element.6, ...), kind=kLoop, calls=%fused_computation.37 | loop fusion | flops 3670016 | bytes 5767168
  68.8 1.5 %fusion.12 = bf16[6,32,64,128]{3,2,1,0:T(8,128)(2,1)} fusion(bf16[6,32,64,128]{3,2,1,0:T(8,128)(2,1)} %fusion.10, f32[32,64,128]{2,1,0:T(8,128)S(1)} %get-tuple-element.9, f32[32,64,128]{2,1,0:T(8,128)S(1)} %get-tuple-element.8, f32[32,64,128]{2,1,0:T(8,128)S(1)} %get-tuple-element.6, f32[34,66,130]{2,1,0:T(8,128)S(1)} %fusion, ...), kind=kLoop, calls=%fused_computation.39 | loop fusion | flops 3932160 | bytes 5767168
  70.3 1.5 %fusion.14 = bf16[6,32,64,128]{3,2,1,0:T(8,128)(2,1)} fusion(bf16[6,32,64,128]{3,2,1,0:T(8,128)(2,1)} %fusion.12, f32[32,64,128]{2,1,0:T(8,128)S(1)} %get-tuple-element.9, f32[32,64,128]{2,1,0:T(8,128)S(1)} %get-tuple-element.8, f32[32,64,128]{2,1,0:T(8,128)S(1)} %get-tuple-element.7, f32[34,66,130]{2,1,0:T(8,128)S(1)} %fusion, ...), kind=kLoop, calls=%fused_computation.41 | loop fusion | flops 3932160 | bytes 5767168
  71.8 1.5 %fusion.16 = bf16[6,32,64,128]{3,2,1,0:T(8,128)(2,1)} fusion(bf16[6,32,64,128]{3,2,1,0:T(8,128)(2,1)} %fusion.14, f32[32,64,128]{2,1,0:T(8,128)S(1)} %get-tuple-element.9, f32[32,64,128]{2,1,0:T(8,128)S(1)} %get-tuple-element.6, f32[32,64,128]{2,1,0:T(8,128)S(1)} %get-tuple-element.7, f32[34,66,130]{2,1,0:T(8,128)S(1)} %fusion, ...), kind=kLoop, calls=%fused_computation.43 | loop fusion | flops 3932160 | bytes 5767168 | tf_op jit(solution)/shard_map/stack | solution.py:49
  (2 shorter events, 0.0 us)
Async XLA Ops:
  8.6 5.3 %collective-permute-start = (f32[2,64,128]{2,1,0:T(8,128)S(1)}, f32[2,64,128]{2,1,0:T(8,128)S(1)}, u32[]{:S(2)}, u32[]{:S(2)}) collective-permute-start(f32[2,64,128]{2,1,0:T(8,128)S(1)} %get-tuple-element.14), channel_id=1, source_target_pairs={{0,64},{64,128},{128,192},{192,256},{256,320},{320,384},{384,448},... | collective-permute-start | bytes 196616 | tf_op jit(solution)/shard_map/ppermute | solution.py:13
  11.7 7.1 %collective-permute-start.1 = (f32[2,64,128]{2,1,0:T(8,128)S(1)}, f32[2,64,128]{2,1,0:T(8,128)S(1)}, u32[]{:S(2)}, u32[]{:S(2)}) collective-permute-start(f32[2,64,128]{2,1,0:T(8,128)S(1)} %get-tuple-element.15), channel_id=1, source_target_pairs={{64,0},{128,64},{192,128},{256,192},{320,256},{384,320},{448,384},... | collective-permute-start | bytes 196616 | tf_op jit(solution)/shard_map/ppermute | solution.py:16
  18.9 12.6 %collective-permute-start.2 = (f32[36,2,128]{2,1,0:T(2,128)S(1)}, f32[36,2,128]{2,1,0:T(2,128)S(1)}, u32[]{:S(2)}, u32[]{:S(2)}) collective-permute-start(f32[36,2,128]{2,1,0:T(2,128)S(1)} %get-tuple-element.12), channel_id=1, source_target_pairs={{0,8},{8,16},{16,24},{24,32},{32,40},{40,48},{48,56},{56,0},{1,9},... | collective-permute-start | bytes 110600 | tf_op jit(solution)/shard_map/ppermute | solution.py:13
  22.9 9.6 %collective-permute-start.3 = (f32[36,2,128]{2,1,0:T(2,128)S(1)}, f32[36,2,128]{2,1,0:T(2,128)S(1)}, u32[]{:S(2)}, u32[]{:S(2)}) collective-permute-start(f32[36,2,128]{2,1,0:T(2,128)S(1)} %get-tuple-element.13), channel_id=1, source_target_pairs={{8,0},{16,8},{24,16},{32,24},{40,32},{48,40},{56,48},{0,56},{9,1},... | collective-permute-start | bytes 110600 | tf_op jit(solution)/shard_map/ppermute | solution.py:16
  36.0 9.8 %collective-permute-start.4 = (f32[36,68,2]{1,2,0:T(2,128)S(1)}, f32[36,68,2]{1,2,0:T(2,128)S(1)}, u32[]{:S(2)}, u32[]{:S(2)}) collective-permute-start(f32[36,68,2]{1,2,0:T(2,128)S(1)} %copy.14), channel_id=1, source_target_pairs={{0,1},{1,2},{2,3},{3,4},{4,5},{5,6},{6,7},{7,0},{8,9},{9,10},{10,1... | collective-permute-start | bytes 58760 | tf_op jit(solution)/shard_map/ppermute | solution.py:13
  43.8 7.4 %collective-permute-start.5 = (f32[36,68,2]{1,2,0:T(2,128)S(1)}, f32[36,68,2]{1,2,0:T(2,128)S(1)}, u32[]{:S(2)}, u32[]{:S(2)}) collective-permute-start(f32[36,68,2]{1,2,0:T(2,128)S(1)} %copy.15), channel_id=1, source_target_pairs={{1,0},{2,1},{3,2},{4,3},{5,4},{6,5},{7,6},{0,7},{9,8},{10,9},{11,1... | collective-permute-start | bytes 58760 | tf_op jit(solution)/shard_map/ppermute | solution.py:16
where the time goes:
time: 73.7 us; the launch traced here: 73.3 us
  other arithmetic  27.6 us (37%)
  starting transfers between devices  27.2 us (37%)
  waiting for transfers between devices  10.8 us (15%)
  local copies, waits for them, and re-layouts  7.55 us (10%)
    ppermute x3, starting transfers between devices, padded_2(): lax.ppermute(lax.slice_in_dim(block, block.shape[dim] - width, None, axis...  14.5 us
    ppermute x3, starting transfers between devices, padded_2(): lax.ppermute(lax.slice_in_dim(block, 0, width, axis=dim), axis, backward)  12.7 us
    unnamed x5, other arithmetic  11.6 us
    ppermute x3, waiting for transfers between devices, padded_2(): lax.ppermute(lax.slice_in_dim(block, 0, width, axis=dim), axis, backward)  10.8 us
    mul x1, other arithmetic, lookup(): return values * grading.astype(jnp.float32)  6.98 us
    slice x3, local copies, waits for them, and re-layouts, padded_2(): lax.slice_in_dim(block, block.shape[dim] - width, None, axis=dim)  3.28 us
    concatenate x2, other arithmetic, padded_2(): block = jnp.concatenate([low, block, high], axis=dim)  2.73 us
    add x2, other arithmetic, box_mean(): total = total[:, :-2] + total[:, 1:-1] + total[:, 2:]  2.23 us
  transfers between devices with their start and end apart: 6, of which 3 were waited for; matrix products, arithmetic and copies ran while one was open for 1% of the time, Pallas kernels for 0%

commit v1 on v0

v1 whole, which is shorter than its diff:
```python
import jax
import jax.numpy as jnp
from jax import lax
from jax.experimental import pallas as pl
from jax.experimental.pallas import tpu as pltpu
from jax.sharding import PartitionSpec as P

F32 = jnp.float32
VMEM = pl.BlockSpec(memory_space=pltpu.VMEM)
SMEM = pl.BlockSpec(memory_space=pltpu.SMEM)
ANY = pl.BlockSpec(memory_space=pl.ANY)


def lookup(material, table, grading):
    low = (material & 1) != 0
    mid = (material & 2) != 0
    top = (material & 4) != 0
    pair = [jnp.where(low, table[2 * k + 1], table[2 * k]) for k in range(4)]
    quad = [jnp.where(mid, pair[2 * k + 1], pair[2 * k]) for k in range(2)]
    return jnp.where(top, quad[1], quad[0]) * grading.astype(F32)


def lanes(shape):
    return lax.broadcasted_iota(jnp.int32, shape, len(shape) - 1)


def scalars(table_ref):
    return [table_ref[k] for k in range(8)]


def faces_kernel(table_ref, mat_low, mat_high, gra_low, gra_high, fwd_ref, bwd_ref):
    table = scalars(table_ref)
    nx = mat_low.shape[0]
    lane = lanes((8, 128))
    packed = [jnp.zeros((8, 128), F32)] * 2
    for x in range(nx):
        low = lookup(mat_low[x], table, gra_low[x, 0:8])
        high = lookup(mat_high[x], table, gra_high[x, 8:16])
        bwd_ref[2 * x : 2 * x + 2] = low[0:2]
        fwd_ref[2 * x : 2 * x + 2] = high[6:8]
        here = (lane >> 2) == x
        turn = (4 * x + 2) % 128
        packed = [
            jnp.where(here, pltpu.roll(v, turn, 1) if turn else v, p)
            for v, p in zip((low, high), packed)
        ]
    ones = jnp.ones((6, 128), F32)
    for ref, rows in ((bwd_ref, packed[0][0:2]), (fwd_ref, packed[1][6:8])):
        ref[2 * nx : 2 * nx + 2] = rows
        ref[2 * nx + 2 : 2 * nx + 8] = ones


def block_kernel(table_ref, mat_ref, gra_ref, eps_ref, packed_ref):
    table = scalars(table_ref)
    step = mat_ref.shape[0]
    first = pl.program_id(0) * step
    lane = lanes(mat_ref.shape[1:])

    @pl.when(first == 0)
    def _():
        packed_ref[...] = jnp.zeros(packed_ref.shape, F32)

    packed = packed_ref[...]
    for k in range(step):
        value = lookup(mat_ref[k], table, gra_ref[k])
        eps_ref[k] = value
        x = first + k
        packed = jnp.where(
            (lane >> 2) == x, pltpu.roll(value, lax.rem(4 * x + 2, 128), 1), packed
        )
    packed_ref[...] = packed


def zface_kernel(packed_ref, low_ref, high_ref, out_ref):
    ny = packed_ref.shape[0]
    out_ref[0:ny] = packed_ref[...]
    out_ref[ny : ny + 2] = low_ref[64:66]
    out_ref[ny + 2 : ny + 4] = high_ref[64:66]
    out_ref[ny + 4 : ny + 8] = jnp.ones((4, 128), F32)


def joined(parity_ref, even_ref, odd_ref):
    lane = lanes(even_ref.shape)
    return jnp.where(((lane >> 1) & 1) == parity_ref[0], odd_ref[...], even_ref[...])


def xface_kernel(parity_ref, eps_ref, low_ref, high_ref, even_ref, odd_ref, fwd_ref, bwd_ref):
    nx, ny = eps_ref.shape[0], eps_ref.shape[1]
    rows = ny + 8
    halo = joined(parity_ref, even_ref, odd_ref)
    lane = lanes((8, 128))
    for ref, start in ((fwd_ref, nx - 2), (bwd_ref, 0)):
        for s in range(2):
            x = start + s
            ref[s * rows : s * rows + ny] = eps_ref[x]
            ref[s * rows + ny : s * rows + ny + 2] = low_ref[2 * x : 2 * x + 2]
            ref[s * rows + ny + 2 : s * rows + ny + 4] = high_ref[2 * x : 2 * x + 2]
            ref[s * rows + ny + 4 : s * rows + rows] = jnp.ones((4, 128), F32)
        packed = jnp.ones((8, 128), F32)
        for g in range(rows // 8):
            turn = (8 * g - 4 * start) % 128
            part = halo[8 * g : 8 * g + 8]
            packed = jnp.where((lane >> 3) == g, pltpu.roll(part, turn, 1) if turn else part, packed)
        ref[2 * rows : 2 * rows + 8] = packed


def zsums(v, h, lane):
    left = pltpu.roll(jnp.where(lane == 127, h, v), 1, 1)
    left2 = pltpu.roll(jnp.where(lane >= 126, h, v), 2, 1)
    right = pltpu.roll(jnp.where(lane == 0, h, v), 127, 1)
    right2 = pltpu.roll(jnp.where(lane <= 1, h, v), 126, 1)
    inv, inv_h = 1.0 / v, 1.0 / h
    inv_left = pltpu.roll(jnp.where(lane == 127, inv_h, inv), 1, 1)
    inv_right = pltpu.roll(jnp.where(lane == 0, inv_h, inv), 127, 1)
    return v + left + right, (right + right2) - (left + left2), inv + inv_left + inv_right


def put(ref, index, value, ny):
    ref[index, 8 : 8 + ny] = value[0:ny]
    ref[index, 6:8] = value[ny : ny + 2]
    ref[index, 8 + ny : 10 + ny] = value[ny + 2 : ny + 4]


def ysums(refs, index, ny):
    box, der, inv = refs
    b = [box[index, 8 + k : 8 + k + ny] for k in (-2, -1, 0, 1, 2)]
    d = [der[index, 8 + k : 8 + k + ny] for k in (-1, 0, 1)]
    i = [inv[index, 8 + k : 8 + k + ny] for k in (-1, 0, 1)]
    return (
        b[1] + b[2] + b[3],
        (b[4] + b[3]) - (b[1] + b[0]),
        d[0] + d[1] + d[2],
        i[0] + i[1] + i[2],
    )


def result(yb, yd, zd, yi):
    mean = yb[1] + yb[2] + yb[3]
    gx = (yb[4] + yb[3]) - (yb[1] + yb[0])
    gy = yd[0] + yd[1] + yd[2]
    gz = zd[0] + zd[1] + zd[2]
    inv = yi[0] + yi[1] + yi[2]
    recip = 27.0 / mean
    factor = (inv * (1.0 / 27.0) - recip) / (gx * gx + gy * gy + gz * gz + 291.6)
    fx, fy, fz = gx * factor, gy * factor, gz * factor
    return (gx * fx + recip, gy * fy + recip, gz * fz + recip, gx * fy, gx * fz, gy * fz)


CHUNK = 4


def inner_kernel(
    parity_ref, eps_ref, low_ref, high_ref, even_ref, odd_ref,
    out_ref, yb_out, yd_out, zd_out, yi_out,
    rim, halo, box, der, inv, yb, yd, zd, yi, obuf, sem,
):
    nx, ny = eps_ref.shape[0], eps_ref.shape[1]
    halo[...] = joined(parity_ref, even_ref, odd_ref)
    lane = lanes((ny + 8, 128))
    ones = jnp.ones((4, 128), F32)
    for x in range(nx):
        rim[x, 0:2] = low_ref[2 * x : 2 * x + 2]
        rim[x, 2:4] = high_ref[2 * x : 2 * x + 2]
        rim[x, 4:8] = ones

    def along_z(x, _):
        v = jnp.concatenate([eps_ref[x], rim[x]], axis=0)
        h = pltpu.roll(halo[...], lax.rem(254 - 4 * x, 128), 1)
        for ref, value in zip((box, der, inv), zsums(v, h, lane)):
            put(ref, x, value, ny)
        return 0

    lax.fori_loop(0, nx, along_z, 0)

    def along_y(x, _):
        for ref, value in zip((yb, yd, zd, yi), ysums((box, der, inv), x, ny)):
            ref[x] = value
        return 0

    lax.fori_loop(0, nx, along_y, 0)
    for ref, out, wide in ((yb, yb_out, 4), (yd, yd_out, 3), (zd, zd_out, 3), (yi, yi_out, 3)):
        out[0:wide] = ref[0:wide]
        out[wide : 2 * wide] = ref[nx - wide : nx]

    def copy(c):
        return pltpu.make_async_copy(
            obuf.at[:, pl.ds(c * CHUNK, CHUNK)], out_ref.at[:, pl.ds(2 + c * CHUNK, CHUNK)], sem.at[c]
        )

    chunks = (nx - 4) // CHUNK

    def along_x(c, _):
        def one(k, _):
            at = c * CHUNK + k
            x = at + 2
            values = result(
                [yb[x + j] for j in (-2, -1, 0, 1, 2)],
                *[[ref[x + j] for j in (-1, 0, 1)] for ref in (yd, zd, yi)],
            )
            for n, value in enumerate(values):
                obuf[n, at] = value.astype(jnp.bfloat16)
            return 0

        lax.fori_loop(0, CHUNK, one, 0)
        copy(c).start()
        return 0

    lax.fori_loop(0, chunks, along_x, 0)

    def finish(c, _):
        copy(c).wait()
        return 0

    lax.fori_loop(0, chunks, finish, 0)


def outer_kernel(
    low_ref, high_ref, yb_in, yd_in, zd_in, yi_in, _, out_ref,
    box, der, inv, yb, yd, zd, yi, obuf, sem,
):
    nx, ny = out_ref.shape[1], out_ref.shape[2]
    rows = ny + 8
    lane = lanes((rows, 128))
    for k, (ref, s) in enumerate(((low_ref, 0), (low_ref, 1), (high_ref, 0), (high_ref, 1))):
        v = ref[s * rows : (s + 1) * rows]
        packed = ref[2 * rows : 2 * rows + 8]
        h = jnp.concatenate(
            [pltpu.roll(packed, (126 - 8 * g - 4 * s) % 128, 1) for g in range(rows // 8)], axis=0
        )
        for dst, value in zip((box, der, inv), zsums(v, h, lane)):
            put(dst, k, value, ny)
    for k in range(4):
        for ref, value in zip((yb, yd, zd, yi), ysums((box, der, inv), k, ny)):
            ref[k] = value
    for side in range(2):
        for s in range(2):
            def pick(halo_ref, own_ref, wide, j):
                x = s + j
                if side == 0:
                    return halo_ref[2 + x] if x < 0 else own_ref[x]
                x = x - 2
                return halo_ref[2 + x] if x >= 0 else own_ref[2 * wide + x]

            values = result(
                [pick(yb, yb_in, 4, j) for j in (-2, -1, 0, 1, 2)],
                *[[pick(h, o, 3, j) for j in (-1, 0, 1)] for h, o in ((yd, yd_in), (zd, zd_in), (yi, yi_in))],
            )
            for n, value in enumerate(values):
                obuf[n, 2 * side + s] = value.astype(jnp.bfloat16)
        pltpu.make_async_copy(
            obuf.at[:, pl.ds(2 * side, 2)], out_ref.at[:, pl.ds(side * (nx - 2), 2)], sem.at[side]
        ).start()
    for side in range(2):
        pltpu.make_async_copy(
            obuf.at[:, pl.ds(2 * side, 2)], out_ref.at[:, pl.ds(side * (nx - 2), 2)], sem.at[side]
        ).wait()


def cost(us):
    return pl.CostEstimate(flops=int(us * 4e6), bytes_accessed=int(us * 1e6), transcendentals=0)


def shape(*dims, dtype=F32):
    return jax.ShapeDtypeStruct(dims, dtype)


def local(material, eps_table, grading):
    nx, ny, nz = material.shape
    rows = ny + 8
    forward = [(i, (i + 1) % 8) for i in range(8)]
    backward = [(b, a) for a, b in forward]
    even = [(i, i ^ 1) for i in range(8)]
    odd = [((i + 1) % 8, ((i ^ 1) + 1) % 8) for i in range(8)]
    parity = (lax.axis_index("gz") & 1).reshape(1)
    vmem = pltpu.CompilerParams(vmem_limit_bytes=24 << 20)

    y_fwd, y_bwd = pl.pallas_call(
        faces_kernel,
        grid=(1,),
        in_specs=[
            SMEM,
            pl.BlockSpec((nx, 8, nz), lambda i: (0, 0, 0)),
            pl.BlockSpec((nx, 8, nz), lambda i: (0, ny // 8 - 1, 0)),
            pl.BlockSpec((nx, 16, nz), lambda i: (0, 0, 0)),
            pl.BlockSpec((nx, 16, nz), lambda i: (0, ny // 16 - 1, 0)),
        ],
        out_specs=[VMEM, VMEM],
        out_shape=[shape(2 * nx + 8, nz)] * 2,
        compiler_params=vmem,
        cost_estimate=cost(1),
        name="faces",
    )(eps_table, material, material, grading, grading)
    y_low = lax.ppermute(y_fwd, "gy", forward)
    y_high = lax.ppermute(y_bwd, "gy", backward)

    step = 8
    eps, packed = pl.pallas_call(
        block_kernel,
        grid=(nx // step,),
        in_specs=[
            SMEM,
            pl.BlockSpec((step, ny, nz), lambda i: (i, 0, 0)),
            pl.BlockSpec((step, ny, nz), lambda i: (i, 0, 0)),
        ],
        out_specs=[
            pl.BlockSpec((step, ny, nz), lambda i: (i, 0, 0)),
            pl.BlockSpec((ny, nz), lambda i: (0, 0)),
        ],
        out_shape=[shape(nx, ny, nz), shape(ny, nz)],
        compiler_params=vmem,
        cost_estimate=cost(3),
        name="block",
    )(eps_table, material, grading)

    z_face = pl.pallas_call(
        zface_kernel,
        in_specs=[VMEM] * 3,
        out_specs=VMEM,
        out_shape=shape(rows, nz),
        compiler_params=vmem,
        cost_estimate=cost(0.2),
        name="zface",
    )(packed, y_low, y_high)
    z_even = lax.ppermute(z_face, "gz", even)
    z_odd = lax.ppermute(z_face, "gz", odd)

    x_fwd, x_bwd = pl.pallas_call(
        xface_kernel,
        in_specs=[SMEM] + [VMEM] * 5,
        out_specs=[VMEM, VMEM],
        out_shape=[shape(2 * rows + 8, nz)] * 2,
        compiler_params=vmem,
        cost_estimate=cost(0.5),
        name="xface",
    )(parity, eps, y_low, y_high, z_even, z_odd)
    x_low = lax.ppermute(x_fwd, "gx", forward)
    x_high = lax.ppermute(x_bwd, "gx", backward)

    full = (nx, ny + 16, nz)
    out, *edges = pl.pallas_call(
        inner_kernel,
        in_specs=[SMEM] + [VMEM] * 5,
        out_specs=[ANY] + [VMEM] * 4,
        out_shape=[shape(6, nx, ny, nz, dtype=jnp.bfloat16), shape(8, ny, nz)]
        + [shape(6, ny, nz)] * 3,
        scratch_shapes=[
            pltpu.VMEM((nx, 8, nz), F32),
            pltpu.VMEM((rows, nz), F32),
            *[pltpu.VMEM(full, F32)] * 3,
            *[pltpu.VMEM((nx, ny, nz), F32)] * 4,
            pltpu.VMEM((6, nx - 4, ny, nz), jnp.bfloat16),
            pltpu.SemaphoreType.DMA(((nx - 4) // CHUNK,)),
        ],
        compiler_params=vmem,
        cost_estimate=cost(6),
        name="inner",
    )(parity, eps, y_low, y_high, z_even, z_odd)

    return pl.pallas_call(
        outer_kernel,
        in_specs=[VMEM] * 6 + [ANY],
        out_specs=ANY,
        out_shape=shape(6, nx, ny, nz, dtype=jnp.bfloat16),
        input_output_aliases={6: 0},
        scratch_shapes=[
            *[pltpu.VMEM((4, ny + 16, nz), F32)] * 3,
            *[pltpu.VMEM((4, ny, nz), F32)] * 4,
            pltpu.VMEM((6, 4, ny, nz), jnp.bfloat16),
            pltpu.SemaphoreType.DMA((2,)),
        ],
        compiler_params=vmem,
        cost_estimate=cost(1),
        name="outer",
    )(x_low, x_high, *edges, out)


def solution(mesh):
    return jax.shard_map(
        local,
        mesh=mesh,
        in_specs=(P("gx", "gy", "gz"), P(), P("gx", "gy", "gz")),
        out_specs=P(None, "gx", "gy", "gz"),
        check_vma=False,
    )
```

time: 73.7 us -> 46 us (0.62)
  the two profiles are of different devices: /device:TPU:23 before, /device:TPU:1 now
where the time goes in v1:
time: 46 us; the launch traced here: 45.7 us
  starting transfers between devices  29 us (63%)
  Pallas kernels  12.8 us (28%)
  local copies, waits for them, and re-layouts  2.92 us (6%)
  waiting for transfers between devices  0.84 us (2%)
    pallas_call x1, Pallas kernels, local(): pl.pallas_call(inner_kernel, in_specs=[SMEM] + [VMEM] * 5, out_specs=[ANY...  9.31 us
    ppermute x1, starting transfers between devices, local(): y_high = lax.ppermute(y_bwd, 'gy', backward)  8.59 us
    ppermute x1, starting transfers between devices, local(): z_odd = lax.ppermute(z_face, 'gz', odd)  5.2 us
    ppermute x1, starting transfers between devices, local(): y_low = lax.ppermute(y_fwd, 'gy', forward)  4.81 us
    ppermute x1, starting transfers between devices, local(): x_high = lax.ppermute(x_bwd, 'gx', backward)  4.27 us
    ppermute x1, starting transfers between devices, local(): x_low = lax.ppermute(x_fwd, 'gx', forward)  3.12 us
    ppermute x1, starting transfers between devices, local(): z_even = lax.ppermute(z_face, 'gz', even)  2.99 us
    unnamed x6, local copies, waits for them, and re-layouts  2.92 us
  transfers between devices with their start and end apart: 6, of which 1 were waited for; matrix products, arithmetic and copies ran while one was open for 0% of the time, Pallas kernels for 23%

profile of v1, /device:TPU:1, one launch (start us, length us, event | category | flops | bytes accessed | tf_op | source)
XLA Modules:
  0.0 45.7 jit_solution(17304587178338262293)
XLA Ops:
  0.0 0.0 copy-start
  0.0 1.2 %copy-done = s32[32,64,128]{2,1,0:T(8,128)S(1)} copy-done((s32[32,64,128]{2,1,0:T(8,128)S(1)}, s32[32,64,128]{2,1,0:T(8,128)}, u32[]{:S(2)}) %copy-start) | copy-done | bytes 1048600
  1.2 0.0 copy-start.1
  1.2 1.0 %copy-done.1 = bf16[32,64,128]{2,1,0:T(8,128)(2,1)S(1)} copy-done((bf16[32,64,128]{2,1,0:T(8,128)(2,1)S(1)}, bf16[32,64,128]{2,1,0:T(8,128)(2,1)}, u32[]{:S(2)}) %copy-start.1) | copy-done | bytes 524312
  2.3 0.0 copy-start.2
  2.3 0.7 %copy-done.2 = f32[8]{0:T(128)S(1)} copy-done((f32[8]{0:T(128)S(1)}, f32[8]{0:T(128)}, u32[]{:S(2)}) %copy-start.2) | copy-done | bytes 56
  2.9 0.7 %faces.1 = (f32[72,128]{1,0:T(8,128)S(1)}, f32[72,128]{1,0:T(8,128)S(1)}) custom-call(f32[8]{0:T(128)S(1)} %copy-done.2, s32[32,64,128]{2,1,0:T(8,128)S(1)} %copy-done, s32[32,64,128]{2,1,0:T(8,128)S(1)} %copy-done, bf16[32,64,128]{2,1,0:T(8,128)(2,1)S(1)} %copy-done.1, bf16[32,64,128]{2,1,0:T(8,128)(2,1)S(1)} %copy-done.1), custom_call_target="tpu_custom_call" | custom-call | flops 4000000 | bytes 1000000 | tf_op jit(solution)/shard_map/faces/pallas_call | solution.py:277
  3.7 4.8 %collective-permute-start = (f32[72,128]{1,0:T(8,128)S(1)}, f32[72,128]{1,0:T(8,128)S(1)}, u32[]{:S(2)}, u32[]{:S(2)}) collective-permute-start(f32[72,128]{1,0:T(8,128)S(1)} %get-tuple-element.17), channel_id=1, source_target_pairs={{0,8},{8,16},{16,24},{24,32},{32,40},{40,48},{48,56},{56,0},{1,9},... | collective-permute-start | bytes 110600 | tf_op jit(solution)/shard_map/ppermute | solution.py:293
  8.5 8.6 %collective-permute-start.1 = (f32[72,128]{1,0:T(8,128)S(1)}, f32[72,128]{1,0:T(8,128)S(1)}, u32[]{:S(2)}, u32[]{:S(2)}) collective-permute-start(f32[72,128]{1,0:T(8,128)S(1)} %get-tuple-element.18), channel_id=1, source_target_pairs={{8,0},{16,8},{24,16},{32,24},{40,32},{48,40},{56,48},{0,56},{9,1},... | collective-permute-start | bytes 110600 | tf_op jit(solution)/shard_map/ppermute | solution.py:294
  17.1 1.4 %block.1 = (f32[32,64,128]{2,1,0:T(8,128)S(1)}, f32[64,128]{1,0:T(8,128)S(1)}) custom-call(f32[8]{0:T(128)S(1)} %copy-done.2, s32[32,64,128]{2,1,0:T(8,128)S(1)} %copy-done, bf16[32,64,128]{2,1,0:T(8,128)(2,1)S(1)} %copy-done.1), custom_call_target="tpu_custom_call" | custom-call | flops 12000000 | bytes 3000000 | tf_op jit(solution)/shard_map/block/pallas_call | solution.py:297
  18.5 0.0 collective-permute-done.low_ref
  18.5 0.0 collective-permute-done.1.high_ref
  18.5 5.2 %collective-permute-start.3 = (f32[72,128]{1,0:T(8,128)S(1)}, f32[72,128]{1,0:T(8,128)S(1)}, u32[]{:S(2)}, u32[]{:S(2)}) collective-permute-start(f32[72,128]{1,0:T(8,128)S(1)} %zface.1), channel_id=1, source_target_pairs={{1,2},{2,1},{3,4},{4,3},{5,6},{6,5},{7,0},{0,7},{9,10},{10,9},{11,... | collective-permute-start | bytes 110600 | tf_op jit(solution)/shard_map/ppermute | solution.py:325
  23.8 3.0 %collective-permute-start.2 = (f32[72,128]{1,0:T(8,128)S(1)}, f32[72,128]{1,0:T(8,128)S(1)}, u32[]{:S(2)}, u32[]{:S(2)}) collective-permute-start(f32[72,128]{1,0:T(8,128)S(1)} %zface.1), channel_id=1, source_target_pairs={{0,1},{1,0},{2,3},{3,2},{4,5},{5,4},{6,7},{7,6},{8,9},{9,8},{10,11... | collective-permute-start | bytes 110600 | tf_op jit(solution)/shard_map/ppermute | solution.py:324
  26.8 0.0 collective-permute-done.3.odd_ref
  26.8 0.8 %collective-permute-done.2.even_ref = f32[72,128]{1,0:T(8,128)S(1)} collective-permute-done((f32[72,128]{1,0:T(8,128)S(1)}, f32[72,128]{1,0:T(8,128)S(1)}, u32[]{:S(2)}, u32[]{:S(2)}) %collective-permute-start.2) | collective-permute-done | bytes 36896 | tf_op jit(solution)/shard_map/ppermute | solution.py:324
  27.6 0.1 xface.1
  27.7 3.1 %collective-permute-start.4 = (f32[152,128]{1,0:T(8,128)S(1)}, f32[152,128]{1,0:T(8,128)S(1)}, u32[]{:S(2)}, u32[]{:S(2)}) collective-permute-start(f32[152,128]{1,0:T(8,128)S(1)} %get-tuple-element.20), channel_id=1, source_target_pairs={{0,64},{64,128},{128,192},{192,256},{256,320},{320,384},{384,448},... | collective-permute-start | bytes 233480 | tf_op jit(solution)/shard_map/ppermute | solution.py:336
  30.8 4.3 %collective-permute-start.5 = (f32[152,128]{1,0:T(8,128)S(1)}, f32[152,128]{1,0:T(8,128)S(1)}, u32[]{:S(2)}, u32[]{:S(2)}) collective-permute-start(f32[152,128]{1,0:T(8,128)S(1)} %get-tuple-element.21), channel_id=1, source_target_pairs={{64,0},{128,64},{192,128},{256,192},{320,256},{384,320},{448,384},... | collective-permute-start | bytes 233480 | tf_op jit(solution)/shard_map/ppermute | solution.py:337
  35.1 9.3 %inner.1 = (bf16[6,32,64,128]{3,2,1,0:T(8,128)(2,1)}, f32[8,64,128]{2,1,0:T(8,128)S(1)}, f32[6,64,128]{2,1,0:T(8,128)S(1)}, f32[6,64,128]{2,1,0:T(8,128)S(1)}, f32[6,64,128]{2,1,0:T(8,128)S(1)}) custom-call(s32[1]{0:T(128)} %bitcast.parity_ref, f32[32,64,128]{2,1,0:T(8,128)S(1)} %get-tuple-element.16.eps_ref, f32[72,128]{1,0:T(8,128)S(1)} %collective-permute-done.low_ref, ...), custom_call_target="tpu_custom_call" | custom-call | flops 24000000 | bytes 6000000 | tf_op jit(solution)/shard_map/inner/pallas_call | solution.py:340
  44.4 0.0 collective-permute-done.4.low_ref
  44.4 0.0 collective-permute-done.5.high_ref
  44.4 1.3 %outer.1 = bf16[6,32,64,128]{3,2,1,0:T(8,128)(2,1)} custom-call(f32[152,128]{1,0:T(8,128)S(1)} %collective-permute-done.4.low_ref, f32[152,128]{1,0:T(8,128)S(1)} %collective-permute-done.5.high_ref, f32[8,64,128]{2,1,0:T(8,128)S(1)} %get-tuple-element.22.yb_in, f32[6,64,128]{2,1,0:T(8,128)S(1)} %get-tuple-element.23.yd_in, ...), custom_call_target="tpu_custom_call", output_to_operand_aliasing={{}: (6, {})} | custom-call | flops 4000000 | bytes 1000000 | tf_op jit(solution)/shard_map/outer/pallas_call | solution.py:359
  (1 shorter events, 0.0 us)
Async XLA Ops:
  0.0 1.2 %copy-start = (s32[32,64,128]{2,1,0:T(8,128)S(1)}, s32[32,64,128]{2,1,0:T(8,128)}, u32[]{:S(2)}) copy-start(s32[32,64,128]{2,1,0:T(8,128)} %mat_high.1) | copy-start | bytes 3145732
  1.2 1.0 %copy-start.1 = (bf16[32,64,128]{2,1,0:T(8,128)(2,1)S(1)}, bf16[32,64,128]{2,1,0:T(8,128)(2,1)}, u32[]{:S(2)}) copy-start(bf16[32,64,128]{2,1,0:T(8,128)(2,1)} %gra_high.1) | copy-start | bytes 1572868
  2.3 0.7 %copy-start.2 = (f32[8]{0:T(128)S(1)}, f32[8]{0:T(128)}, u32[]{:S(2)}) copy-start(f32[8]{0:T(128)} %table_ref.3) | copy-start | bytes 100
  3.7 14.9 %collective-permute-start = (f32[72,128]{1,0:T(8,128)S(1)}, f32[72,128]{1,0:T(8,128)S(1)}, u32[]{:S(2)}, u32[]{:S(2)}) collective-permute-start(f32[72,128]{1,0:T(8,128)S(1)} %get-tuple-element.17), channel_id=1, source_target_pairs={{0,8},{8,16},{16,24},{24,32},{32,40},{40,48},{48,56},{56,0},{1,9},... | collective-permute-start | bytes 110600 | tf_op jit(solution)/shard_map/ppermute | solution.py:293
  8.5 10.0 %collective-permute-start.1 = (f32[72,128]{1,0:T(8,128)S(1)}, f32[72,128]{1,0:T(8,128)S(1)}, u32[]{:S(2)}, u32[]{:S(2)}) collective-permute-start(f32[72,128]{1,0:T(8,128)S(1)} %get-tuple-element.18), channel_id=1, source_target_pairs={{8,0},{16,8},{24,16},{32,24},{40,32},{48,40},{56,48},{0,56},{9,1},... | collective-permute-start | bytes 110600 | tf_op jit(solution)/shard_map/ppermute | solution.py:294
  18.5 8.2 %collective-permute-start.3 = (f32[72,128]{1,0:T(8,128)S(1)}, f32[72,128]{1,0:T(8,128)S(1)}, u32[]{:S(2)}, u32[]{:S(2)}) collective-permute-start(f32[72,128]{1,0:T(8,128)S(1)} %zface.1), channel_id=1, source_target_pairs={{1,2},{2,1},{3,4},{4,3},{5,6},{6,5},{7,0},{0,7},{9,10},{10,9},{11,... | collective-permute-start | bytes 110600 | tf_op jit(solution)/shard_map/ppermute | solution.py:325
  23.8 3.8 %collective-permute-start.2 = (f32[72,128]{1,0:T(8,128)S(1)}, f32[72,128]{1,0:T(8,128)S(1)}, u32[]{:S(2)}, u32[]{:S(2)}) collective-permute-start(f32[72,128]{1,0:T(8,128)S(1)} %zface.1), channel_id=1, source_target_pairs={{0,1},{1,0},{2,3},{3,2},{4,5},{5,4},{6,7},{7,6},{8,9},{9,8},{10,11... | collective-permute-start | bytes 110600 | tf_op jit(solution)/shard_map/ppermute | solution.py:324
  27.7 16.7 %collective-permute-start.4 = (f32[152,128]{1,0:T(8,128)S(1)}, f32[152,128]{1,0:T(8,128)S(1)}, u32[]{:S(2)}, u32[]{:S(2)}) collective-permute-start(f32[152,128]{1,0:T(8,128)S(1)} %get-tuple-element.20), channel_id=1, source_target_pairs={{0,64},{64,128},{128,192},{192,256},{256,320},{320,384},{384,448},... | collective-permute-start | bytes 233480 | tf_op jit(solution)/shard_map/ppermute | solution.py:336
  30.8 13.6 %collective-permute-start.5 = (f32[152,128]{1,0:T(8,128)S(1)}, f32[152,128]{1,0:T(8,128)S(1)}, u32[]{:S(2)}, u32[]{:S(2)}) collective-permute-start(f32[152,128]{1,0:T(8,128)S(1)} %get-tuple-element.21), channel_id=1, source_target_pairs={{64,0},{128,64},{192,128},{256,192},{320,256},{384,320},{448,384},... | collective-permute-start | bytes 233480 | tf_op jit(solution)/shard_map/ppermute | solution.py:337

commit v2 on v1

--- a/solution.py
+++ b/solution.py
@@ -9,6 +9,7 @@
 VMEM = pl.BlockSpec(memory_space=pltpu.VMEM)
 SMEM = pl.BlockSpec(memory_space=pltpu.SMEM)
 ANY = pl.BlockSpec(memory_space=pl.ANY)
+HBM = pl.BlockSpec(memory_space=pltpu.HBM)
 
 
 def lookup(material, table, grading):
@@ -28,9 +29,28 @@
     return [table_ref[k] for k in range(8)]
 
 
-def faces_kernel(table_ref, mat_low, mat_high, gra_low, gra_high, fwd_ref, bwd_ref):
+def faces_kernel(
+    table_hbm, mat_hbm, gra_hbm, fwd_ref, bwd_ref,
+    table_ref, mat_low, mat_high, gra_low, gra_high, sem,
+):
+    nx, ny = mat_hbm.shape[0], mat_hbm.shape[1]
+    copies = [
+        pltpu.make_async_copy(src, dst, sem.at[k])
+        for k, (src, dst) in enumerate(
+            (
+                (mat_hbm.at[:, 0:8], mat_low),
+                (mat_hbm.at[:, ny - 8 : ny], mat_high),
+                (gra_hbm.at[:, 0:16], gra_low),
+                (gra_hbm.at[:, ny - 16 : ny], gra_high),
+                (table_hbm, table_ref),
+            )
+        )
+    ]
+    for copy in copies:
+        copy.start()
+    for copy in copies:
+        copy.wait()
     table = scalars(table_ref)
-    nx = mat_low.shape[0]
     lane = lanes((8, 128))
     packed = [jnp.zeros((8, 128), F32)] * 2
     for x in range(nx):
@@ -50,25 +70,41 @@
         ref[2 * nx + 2 : 2 * nx + 8] = ones
 
 
-def block_kernel(table_ref, mat_ref, gra_ref, eps_ref, packed_ref):
+STEP = 8
+
+
+def block_kernel(table_hbm, mat_hbm, gra_hbm, eps_ref, packed_ref, table_ref, mat_ref, gra_ref, sem):
+    nx, ny = mat_hbm.shape[0], mat_hbm.shape[1]
+
+    def copies(c):
+        part = pl.ds(c * STEP, STEP)
+        return (
+            pltpu.make_async_copy(mat_hbm.at[part], mat_ref.at[part], sem.at[0, c]),
+            pltpu.make_async_copy(gra_hbm.at[part], gra_ref.at[part], sem.at[1, c]),
+        )
+
+    first = pltpu.make_async_copy(table_hbm, table_ref, sem.at[2, 0])
+    first.start()
+    for c in range(nx // STEP):
+        for copy in copies(c):
+            copy.start()
+    first.wait()
     table = scalars(table_ref)
-    step = mat_ref.shape[0]
-    first = pl.program_id(0) * step
-    lane = lanes(mat_ref.shape[1:])
-
-    @pl.when(first == 0)
-    def _():
-        packed_ref[...] = jnp.zeros(packed_ref.shape, F32)
-
-    packed = packed_ref[...]
-    for k in range(step):
-        value = lookup(mat_ref[k], table, gra_ref[k])
-        eps_ref[k] = value
-        x = first + k
-        packed = jnp.where(
-            (lane >> 2) == x, pltpu.roll(value, lax.rem(4 * x + 2, 128), 1), packed
-        )
-    packed_ref[...] = packed
+    lane = lanes((ny, 128))
+
+    def one(c, packed):
+        for copy in copies(c):
+            copy.wait()
+        for k in range(STEP):
+            x = c * STEP + k
+            value = lookup(mat_ref[x], table, gra_ref[x])
+            eps_ref[x] = value
+            packed = jnp.where(
+                (lane >> 2) == x, pltpu.roll(value, lax.rem(4 * x + 2, 128), 1), packed
+            )
+        return packed
+
+    packed_ref[...] = lax.fori_loop(0, nx // STEP, one, jnp.zeros((ny, 128), F32))
 
 
 def zface_kernel(packed_ref, low_ref, high_ref, out_ref):
@@ -121,11 +157,11 @@
     ref[index, 8 + ny : 10 + ny] = value[ny + 2 : ny + 4]
 
 
-def ysums(refs, index, ny):
+def ysums(refs, index, count, r):
     box, der, inv = refs
-    b = [box[index, 8 + k : 8 + k + ny] for k in (-2, -1, 0, 1, 2)]
-    d = [der[index, 8 + k : 8 + k + ny] for k in (-1, 0, 1)]
-    i = [inv[index, 8 + k : 8 + k + ny] for k in (-1, 0, 1)]
+    b = [box[index, 8 + r + k : 8 + r + k + count] for k in (-2, -1, 0, 1, 2)]
+    d = [der[index, 8 + r + k : 8 + r + k + count] for k in (-1, 0, 1)]
+    i = [inv[index, 8 + r + k : 8 + r + k + count] for k in (-1, 0, 1)]
     return (
         b[1] + b[2] + b[3],
         (b[4] + b[3]) - (b[1] + b[0]),
@@ -147,12 +183,13 @@
 
 
 CHUNK = 4
+UNROLL = 4
 
 
 def inner_kernel(
     parity_ref, eps_ref, low_ref, high_ref, even_ref, odd_ref,
     out_ref, yb_out, yd_out, zd_out, yi_out,
-    rim, halo, box, der, inv, yb, yd, zd, yi, obuf, sem,
+    rim, halo, side, box, der, inv, yb, yd, zd, yi, obuf, sem,
 ):
     nx, ny = eps_ref.shape[0], eps_ref.shape[1]
     halo[...] = joined(parity_ref, even_ref, odd_ref)
@@ -163,18 +200,28 @@
         rim[x, 2:4] = high_ref[2 * x : 2 * x + 2]
         rim[x, 4:8] = ones
 
-    def along_z(x, _):
-        v = jnp.concatenate([eps_ref[x], rim[x]], axis=0)
-        h = pltpu.roll(halo[...], lax.rem(254 - 4 * x, 128), 1)
-        for ref, value in zip((box, der, inv), zsums(v, h, lane)):
-            put(ref, x, value, ny)
+    def turned(c, _):
+        for k in range(UNROLL):
+            x = c * UNROLL + k
+            side[x] = pltpu.roll(halo[...], lax.rem(254 - 4 * x, 128), 1)
         return 0
 
-    lax.fori_loop(0, nx, along_z, 0)
+    lax.fori_loop(0, nx // UNROLL, turned, 0)
+
+    def along_z(c, _):
+        for k in range(UNROLL):
+            x = c * UNROLL + k
+            v = jnp.concatenate([eps_ref[x], rim[x]], axis=0)
+            for ref, value in zip((box, der, inv), zsums(v, side[x], lane)):
+                put(ref, x, value, ny)
+        return 0
+
+    lax.fori_loop(0, nx // UNROLL, along_z, 0)
 
     def along_y(x, _):
-        for ref, value in zip((yb, yd, zd, yi), ysums((box, der, inv), x, ny)):
-            ref[x] = value
+        for r in range(0, ny, 16):
+            for ref, value in zip((yb, yd, zd, yi), ysums((box, der, inv), x, 16, r)):
+                ref[x, r : r + 16] = value
         return 0
 
     lax.fori_loop(0, nx, along_y, 0)
@@ -193,12 +240,14 @@
         def one(k, _):
             at = c * CHUNK + k
             x = at + 2
-            values = result(
-                [yb[x + j] for j in (-2, -1, 0, 1, 2)],
-                *[[ref[x + j] for j in (-1, 0, 1)] for ref in (yd, zd, yi)],
-            )
-            for n, value in enumerate(values):
-                obuf[n, at] = value.astype(jnp.bfloat16)
+            for r in range(0, ny, 16):
+                part = slice(r, r + 16)
+                values = result(
+                    [yb[x + j, part] for j in (-2, -1, 0, 1, 2)],
+                    *[[ref[x + j, part] for j in (-1, 0, 1)] for ref in (yd, zd, yi)],
+                )
+                for n, value in enumerate(values):
+                    obuf[n, at, part] = value.astype(jnp.bfloat16)
             return 0
 
         lax.fori_loop(0, CHUNK, one, 0)
@@ -230,23 +279,29 @@
         for dst, value in zip((box, der, inv), zsums(v, h, lane)):
             put(dst, k, value, ny)
     for k in range(4):
-        for ref, value in zip((yb, yd, zd, yi), ysums((box, der, inv), k, ny)):
-            ref[k] = value
+        for r in range(0, ny, 16):
+            for ref, value in zip((yb, yd, zd, yi), ysums((box, der, inv), k, 16, r)):
+                ref[k, r : r + 16] = value
     for side in range(2):
         for s in range(2):
-            def pick(halo_ref, own_ref, wide, j):
+            def pick(halo_ref, own_ref, wide, j, part):
                 x = s + j
                 if side == 0:
-                    return halo_ref[2 + x] if x < 0 else own_ref[x]
+                    return halo_ref[2 + x, part] if x < 0 else own_ref[x, part]
                 x = x - 2
-                return halo_ref[2 + x] if x >= 0 else own_ref[2 * wide + x]
-
-            values = result(
-                [pick(yb, yb_in, 4, j) for j in (-2, -1, 0, 1, 2)],
-                *[[pick(h, o, 3, j) for j in (-1, 0, 1)] for h, o in ((yd, yd_in), (zd, zd_in), (yi, yi_in))],
-            )
-            for n, value in enumerate(values):
-                obuf[n, 2 * side + s] = value.astype(jnp.bfloat16)
+                return halo_ref[2 + x, part] if x >= 0 else own_ref[2 * wide + x, part]
+
+            for r in range(0, ny, 16):
+                part = slice(r, r + 16)
+                values = result(
+                    [pick(yb, yb_in, 4, j, part) for j in (-2, -1, 0, 1, 2)],
+                    *[
+                        [pick(h, o, 3, j, part) for j in (-1, 0, 1)]
+                        for h, o in ((yd, yd_in), (zd, zd_in), (yi, yi_in))
+                    ],
+                )
+                for n, value in enumerate(values):
+                    obuf[n, 2 * side + s, part] = value.astype(jnp.bfloat16)
         pltpu.make_async_copy(
             obuf.at[:, pl.ds(2 * side, 2)], out_ref.at[:, pl.ds(side * (nx - 2), 2)], sem.at[side]
         ).start()
@@ -267,6 +322,9 @@
 def local(material, eps_table, grading):
     nx, ny, nz = material.shape
     rows = ny + 8
+    material, eps_table, grading = (
+        pltpu.with_memory_space_constraint(a, pltpu.HBM) for a in (material, eps_table, grading)
+    )
     forward = [(i, (i + 1) % 8) for i in range(8)]
     backward = [(b, a) for a, b in forward]
     even = [(i, i ^ 1) for i in range(8)]
@@ -276,37 +334,33 @@
 
     y_fwd, y_bwd = pl.pallas_call(
         faces_kernel,
-        grid=(1,),
-        in_specs=[
-            SMEM,
-            pl.BlockSpec((nx, 8, nz), lambda i: (0, 0, 0)),
-            pl.BlockSpec((nx, 8, nz), lambda i: (0, ny // 8 - 1, 0)),
-            pl.BlockSpec((nx, 16, nz), lambda i: (0, 0, 0)),
-            pl.BlockSpec((nx, 16, nz), lambda i: (0, ny // 16 - 1, 0)),
-        ],
+        in_specs=[HBM] * 3,
         out_specs=[VMEM, VMEM],
         out_shape=[shape(2 * nx + 8, nz)] * 2,
+        scratch_shapes=[
+            pltpu.SMEM((8,), F32),
+            *[pltpu.VMEM((nx, 8, nz), jnp.int32)] * 2,
+            *[pltpu.VMEM((nx, 16, nz), jnp.bfloat16)] * 2,
+            pltpu.SemaphoreType.DMA((5,)),
+        ],
         compiler_params=vmem,
         cost_estimate=cost(1),
         name="faces",
-    )(eps_table, material, material, grading, grading)
+    )(eps_table, material, grading)
     y_low = lax.ppermute(y_fwd, "gy", forward)
     y_high = lax.ppermute(y_bwd, "gy", backward)
 
-    step = 8
     eps, packed = pl.pallas_call(
         block_kernel,
-        grid=(nx // step,),
-        in_specs=[
-            SMEM,
-            pl.BlockSpec((step, ny, nz), lambda i: (i, 0, 0)),
-            pl.BlockSpec((step, ny, nz), lambda i: (i, 0, 0)),
+        in_specs=[HBM] * 3,
+        out_specs=[VMEM, VMEM],
+        out_shape=[shape(nx, ny, nz), shape(ny, nz)],
+        scratch_shapes=[
+            pltpu.SMEM((8,), F32),
+            pltpu.VMEM((nx, ny, nz), jnp.int32),
+            pltpu.VMEM((nx, ny, nz), jnp.bfloat16),
+            pltpu.SemaphoreType.DMA((3, nx // STEP)),
         ],
-        out_specs=[
-            pl.BlockSpec((step, ny, nz), lambda i: (i, 0, 0)),
-            pl.BlockSpec((ny, nz), lambda i: (0, 0)),
-        ],
-        out_shape=[shape(nx, ny, nz), shape(ny, nz)],
         compiler_params=vmem,
         cost_estimate=cost(3),
         name="block",
@@ -346,6 +400,7 @@
         scratch_shapes=[
             pltpu.VMEM((nx, 8, nz), F32),
             pltpu.VMEM((rows, nz), F32),
+            pltpu.VMEM((nx, rows, nz), F32),
             *[pltpu.VMEM(full, F32)] * 3,
             *[pltpu.VMEM((nx, ny, nz), F32)] * 4,
             pltpu.VMEM((6, nx - 4, ny, nz), jnp.bfloat16),

time: 46 us -> 41.2 us (0.90)
  local copies, waits for them, and re-layouts: 2.92 us -> 0 us
  Pallas kernels: 12.8 us -> 11 us
    pallas_call x1, Pallas kernels: 9.31 us -> 6.36 us  [local(): pl.pallas_call(inner_kernel, in_specs=[SMEM] + [VMEM] * 5, out_specs=[ANY...]
    unnamed x6 -> x0, local copies, waits for them, and re-layouts: 2.92 us -> none
    pallas_call x2, Pallas kernels: 2.16 us -> 3.24 us  [the longest x1 1.9 us: local(): pl.pallas_call(block_kernel, in_specs=[HBM] * 3, out_specs=[VMEM, VMEM],...]
  transfers between devices with their start and end apart: 6 -> 6, of which waited for: 1 -> 1; matrix products, arithmetic and copies ran while one was open for 0% -> 0% of each run, Pallas kernels for 23% -> 20%
where the time goes in v2:
time: 41.2 us; the launch traced here: 40.9 us
  starting transfers between devices  29 us (70%)
  Pallas kernels  11 us (27%)
  waiting for transfers between devices  0.84 us (2%)
    ppermute x1, starting transfers between devices, local(): y_high = lax.ppermute(y_bwd, 'gy', backward)  8.59 us
    pallas_call x1, Pallas kernels, local(): pl.pallas_call(inner_kernel, in_specs=[SMEM] + [VMEM] * 5, out_specs=[ANY...  6.36 us
    ppermute x1, starting transfers between devices, local(): z_odd = lax.ppermute(z_face, 'gz', odd)  5.06 us
    ppermute x1, starting transfers between devices, local(): y_low = lax.ppermute(y_fwd, 'gy', forward)  4.82 us
    ppermute x1, starting transfers between devices, local(): x_high = lax.ppermute(x_bwd, 'gx', backward)  4.27 us
    ppermute x1, starting transfers between devices, local(): z_even = lax.ppermute(z_face, 'gz', even)  3.13 us
    ppermute x1, starting transfers between devices, local(): x_low = lax.ppermute(x_fwd, 'gx', forward)  3.12 us
    pallas_call x1, Pallas kernels, local(): pl.pallas_call(block_kernel, in_specs=[HBM] * 3, out_specs=[VMEM, VMEM],...  1.9 us
  transfers between devices with their start and end apart: 6, of which 1 were waited for; matrix products, arithmetic and copies ran while one was open for 0% of the time, Pallas kernels for 20%

profile of v2, /device:TPU:1, one launch (start us, length us, event | category | flops | bytes accessed | tf_op | source)
XLA Modules:
  0.0 40.9 jit_solution(1658891417056387975)
XLA Ops:
  0.0 1.3 %faces.1 = (f32[72,128]{1,0:T(8,128)S(1)}, f32[72,128]{1,0:T(8,128)S(1)}) custom-call(f32[8]{0:T(128)} %table_hbm.3, s32[32,64,128]{2,1,0:T(8,128)} %mat_hbm.3, bf16[32,64,128]{2,1,0:T(8,128)(2,1)} %gra_hbm.3), custom_call_target="tpu_custom_call" | custom-call | flops 4000000 | bytes 1000000 | tf_op jit(solution)/shard_map/faces/pallas_call | solution.py:335
  1.4 4.8 %collective-permute-start = (f32[72,128]{1,0:T(8,128)S(1)}, f32[72,128]{1,0:T(8,128)S(1)}, u32[]{:S(2)}, u32[]{:S(2)}) collective-permute-start(f32[72,128]{1,0:T(8,128)S(1)} %get-tuple-element.17), channel_id=1, source_target_pairs={{0,8},{8,16},{16,24},{24,32},{32,40},{40,48},{48,56},{56,0},{1,9},... | collective-permute-start | bytes 110600 | tf_op jit(solution)/shard_map/ppermute | solution.py:350
  6.2 8.6 %collective-permute-start.1 = (f32[72,128]{1,0:T(8,128)S(1)}, f32[72,128]{1,0:T(8,128)S(1)}, u32[]{:S(2)}, u32[]{:S(2)}) collective-permute-start(f32[72,128]{1,0:T(8,128)S(1)} %get-tuple-element.18), channel_id=1, source_target_pairs={{8,0},{16,8},{24,16},{32,24},{40,32},{48,40},{56,48},{0,56},{9,1},... | collective-permute-start | bytes 110600 | tf_op jit(solution)/shard_map/ppermute | solution.py:351
  14.8 1.9 %block.1 = (f32[32,64,128]{2,1,0:T(8,128)S(1)}, f32[64,128]{1,0:T(8,128)S(1)}) custom-call(f32[8]{0:T(128)} %table_hbm.3, s32[32,64,128]{2,1,0:T(8,128)} %mat_hbm.3, bf16[32,64,128]{2,1,0:T(8,128)(2,1)} %gra_hbm.3), custom_call_target="tpu_custom_call" | custom-call | flops 12000000 | bytes 3000000 | tf_op jit(solution)/shard_map/block/pallas_call | solution.py:353
  16.7 0.0 collective-permute-done.low_ref
  16.7 0.0 collective-permute-done.1.high_ref
  16.7 5.1 %collective-permute-start.3 = (f32[72,128]{1,0:T(8,128)S(1)}, f32[72,128]{1,0:T(8,128)S(1)}, u32[]{:S(2)}, u32[]{:S(2)}) collective-permute-start(f32[72,128]{1,0:T(8,128)S(1)} %zface.1), channel_id=1, source_target_pairs={{1,2},{2,1},{3,4},{4,3},{5,6},{6,5},{7,0},{0,7},{9,10},{10,9},{11,... | collective-permute-start | bytes 110600 | tf_op jit(solution)/shard_map/ppermute | solution.py:379
  21.8 3.1 %collective-permute-start.2 = (f32[72,128]{1,0:T(8,128)S(1)}, f32[72,128]{1,0:T(8,128)S(1)}, u32[]{:S(2)}, u32[]{:S(2)}) collective-permute-start(f32[72,128]{1,0:T(8,128)S(1)} %zface.1), channel_id=1, source_target_pairs={{0,1},{1,0},{2,3},{3,2},{4,5},{5,4},{6,7},{7,6},{8,9},{9,8},{10,11... | collective-permute-start | bytes 110600 | tf_op jit(solution)/shard_map/ppermute | solution.py:378
  24.9 0.0 collective-permute-done.3.odd_ref
  24.9 0.8 %collective-permute-done.2.even_ref = f32[72,128]{1,0:T(8,128)S(1)} collective-permute-done((f32[72,128]{1,0:T(8,128)S(1)}, f32[72,128]{1,0:T(8,128)S(1)}, u32[]{:S(2)}, u32[]{:S(2)}) %collective-permute-start.2) | collective-permute-done | bytes 36896 | tf_op jit(solution)/shard_map/ppermute | solution.py:378
  25.8 0.1 xface.1
  25.9 3.1 %collective-permute-start.4 = (f32[152,128]{1,0:T(8,128)S(1)}, f32[152,128]{1,0:T(8,128)S(1)}, u32[]{:S(2)}, u32[]{:S(2)}) collective-permute-start(f32[152,128]{1,0:T(8,128)S(1)} %get-tuple-element.20), channel_id=1, source_target_pairs={{0,64},{64,128},{128,192},{192,256},{256,320},{320,384},{384,448},... | collective-permute-start | bytes 233480 | tf_op jit(solution)/shard_map/ppermute | solution.py:390
  29.0 4.3 %collective-permute-start.5 = (f32[152,128]{1,0:T(8,128)S(1)}, f32[152,128]{1,0:T(8,128)S(1)}, u32[]{:S(2)}, u32[]{:S(2)}) collective-permute-start(f32[152,128]{1,0:T(8,128)S(1)} %get-tuple-element.21), channel_id=1, source_target_pairs={{64,0},{128,64},{192,128},{256,192},{320,256},{384,320},{448,384},... | collective-permute-start | bytes 233480 | tf_op jit(solution)/shard_map/ppermute | solution.py:391
  33.3 6.4 %inner.1 = (bf16[6,32,64,128]{3,2,1,0:T(8,128)(2,1)}, f32[8,64,128]{2,1,0:T(8,128)S(1)}, f32[6,64,128]{2,1,0:T(8,128)S(1)}, f32[6,64,128]{2,1,0:T(8,128)S(1)}, f32[6,64,128]{2,1,0:T(8,128)S(1)}) custom-call(s32[1]{0:T(128)} %bitcast.parity_ref, f32[32,64,128]{2,1,0:T(8,128)S(1)} %get-tuple-element.16.eps_ref, f32[72,128]{1,0:T(8,128)S(1)} %collective-permute-done.low_ref, ...), custom_call_target="tpu_custom_call" | custom-call | flops 24000000 | bytes 6000000 | tf_op jit(solution)/shard_map/inner/pallas_call | solution.py:394
  39.6 0.0 collective-permute-done.4.low_ref
  39.6 0.0 collective-permute-done.5.high_ref
  39.6 1.3 %outer.1 = bf16[6,32,64,128]{3,2,1,0:T(8,128)(2,1)} custom-call(f32[152,128]{1,0:T(8,128)S(1)} %collective-permute-done.4.low_ref, f32[152,128]{1,0:T(8,128)S(1)} %collective-permute-done.5.high_ref, f32[8,64,128]{2,1,0:T(8,128)S(1)} %get-tuple-element.22.yb_in, f32[6,64,128]{2,1,0:T(8,128)S(1)} %get-tuple-element.23.yd_in, ...), custom_call_target="tpu_custom_call", output_to_operand_aliasing={{}: (6, {})} | custom-call | flops 4000000 | bytes 1000000 | tf_op jit(solution)/shard_map/outer/pallas_call | solution.py:414
  (1 shorter events, 0.0 us)
Async XLA Ops:
  1.4 15.3 %collective-permute-start = (f32[72,128]{1,0:T(8,128)S(1)}, f32[72,128]{1,0:T(8,128)S(1)}, u32[]{:S(2)}, u32[]{:S(2)}) collective-permute-start(f32[72,128]{1,0:T(8,128)S(1)} %get-tuple-element.17), channel_id=1, source_target_pairs={{0,8},{8,16},{16,24},{24,32},{32,40},{40,48},{48,56},{56,0},{1,9},... | collective-permute-start | bytes 110600 | tf_op jit(solution)/shard_map/ppermute | solution.py:350
  6.2 10.5 %collective-permute-start.1 = (f32[72,128]{1,0:T(8,128)S(1)}, f32[72,128]{1,0:T(8,128)S(1)}, u32[]{:S(2)}, u32[]{:S(2)}) collective-permute-start(f32[72,128]{1,0:T(8,128)S(1)} %get-tuple-element.18), channel_id=1, source_target_pairs={{8,0},{16,8},{24,16},{32,24},{40,32},{48,40},{56,48},{0,56},{9,1},... | collective-permute-start | bytes 110600 | tf_op jit(solution)/shard_map/ppermute | solution.py:351
  16.7 8.2 %collective-permute-start.3 = (f32[72,128]{1,0:T(8,128)S(1)}, f32[72,128]{1,0:T(8,128)S(1)}, u32[]{:S(2)}, u32[]{:S(2)}) collective-permute-start(f32[72,128]{1,0:T(8,128)S(1)} %zface.1), channel_id=1, source_target_pairs={{1,2},{2,1},{3,4},{4,3},{5,6},{6,5},{7,0},{0,7},{9,10},{10,9},{11,... | collective-permute-start | bytes 110600 | tf_op jit(solution)/shard_map/ppermute | solution.py:379
  21.8 4.0 %collective-permute-start.2 = (f32[72,128]{1,0:T(8,128)S(1)}, f32[72,128]{1,0:T(8,128)S(1)}, u32[]{:S(2)}, u32[]{:S(2)}) collective-permute-start(f32[72,128]{1,0:T(8,128)S(1)} %zface.1), channel_id=1, source_target_pairs={{0,1},{1,0},{2,3},{3,2},{4,5},{5,4},{6,7},{7,6},{8,9},{9,8},{10,11... | collective-permute-start | bytes 110600 | tf_op jit(solution)/shard_map/ppermute | solution.py:378
  25.9 13.8 %collective-permute-start.4 = (f32[152,128]{1,0:T(8,128)S(1)}, f32[152,128]{1,0:T(8,128)S(1)}, u32[]{:S(2)}, u32[]{:S(2)}) collective-permute-start(f32[152,128]{1,0:T(8,128)S(1)} %get-tuple-element.20), channel_id=1, source_target_pairs={{0,64},{64,128},{128,192},{192,256},{256,320},{320,384},{384,448},... | collective-permute-start | bytes 233480 | tf_op jit(solution)/shard_map/ppermute | solution.py:390
  29.0 10.7 %collective-permute-start.5 = (f32[152,128]{1,0:T(8,128)S(1)}, f32[152,128]{1,0:T(8,128)S(1)}, u32[]{:S(2)}, u32[]{:S(2)}) collective-permute-start(f32[152,128]{1,0:T(8,128)S(1)} %get-tuple-element.21), channel_id=1, source_target_pairs={{64,0},{128,64},{192,128},{256,192},{320,256},{384,320},{448,384},... | collective-permute-start | bytes 233480 | tf_op jit(solution)/shard_map/ppermute | solution.py:391

commit v3 on v2

--- a/solution.py
+++ b/solution.py
@@ -29,8 +29,13 @@
     return [table_ref[k] for k in range(8)]
 
 
-def faces_kernel(
-    table_hbm, mat_hbm, gra_hbm, fwd_ref, bwd_ref,
+def finish_face(ref, rows, nx):
+    ref[2 * nx : 2 * nx + 2] = rows
+    ref[2 * nx + 2 : 2 * nx + 8] = jnp.ones((6, 128), F32)
+
+
+def face_kernel(
+    table_hbm, mat_hbm, gra_hbm, fwd_ref, bwd_ref, mat_ref, gra_ref, rows_ref,
     table_ref, mat_low, mat_high, gra_low, gra_high, sem,
 ):
     nx, ny = mat_hbm.shape[0], mat_hbm.shape[1]
@@ -38,19 +43,23 @@
         pltpu.make_async_copy(src, dst, sem.at[k])
         for k, (src, dst) in enumerate(
             (
+                (table_hbm, table_ref),
                 (mat_hbm.at[:, 0:8], mat_low),
+                (gra_hbm.at[:, 0:16], gra_low),
                 (mat_hbm.at[:, ny - 8 : ny], mat_high),
-                (gra_hbm.at[:, 0:16], gra_low),
                 (gra_hbm.at[:, ny - 16 : ny], gra_high),
-                (table_hbm, table_ref),
+                (mat_hbm, mat_ref),
+                (gra_hbm, gra_ref),
             )
         )
     ]
     for copy in copies:
         copy.start()
-    for copy in copies:
+    for copy in copies[:5]:
         copy.wait()
     table = scalars(table_ref)
+    for k in range(8):
+        rows_ref[k : k + 1] = jnp.full((1, 128), table[k], F32)
     lane = lanes((8, 128))
     packed = [jnp.zeros((8, 128), F32)] * 2
     for x in range(nx):
@@ -58,43 +67,26 @@
         high = lookup(mat_high[x], table, gra_high[x, 8:16])
         bwd_ref[2 * x : 2 * x + 2] = low[0:2]
         fwd_ref[2 * x : 2 * x + 2] = high[6:8]
-        here = (lane >> 2) == x
         turn = (4 * x + 2) % 128
         packed = [
-            jnp.where(here, pltpu.roll(v, turn, 1) if turn else v, p)
+            jnp.where((lane >> 2) == x, pltpu.roll(v, turn, 1) if turn else v, p)
             for v, p in zip((low, high), packed)
         ]
-    ones = jnp.ones((6, 128), F32)
-    for ref, rows in ((bwd_ref, packed[0][0:2]), (fwd_ref, packed[1][6:8])):
-        ref[2 * nx : 2 * nx + 2] = rows
-        ref[2 * nx + 2 : 2 * nx + 8] = ones
+    finish_face(bwd_ref, packed[0][0:2], nx)
+    finish_face(fwd_ref, packed[1][6:8], nx)
+    for copy in copies[5:]:
+        copy.wait()
 
 
 STEP = 8
 
 
-def block_kernel(table_hbm, mat_hbm, gra_hbm, eps_ref, packed_ref, table_ref, mat_ref, gra_ref, sem):
-    nx, ny = mat_hbm.shape[0], mat_hbm.shape[1]
-
-    def copies(c):
-        part = pl.ds(c * STEP, STEP)
-        return (
-            pltpu.make_async_copy(mat_hbm.at[part], mat_ref.at[part], sem.at[0, c]),
-            pltpu.make_async_copy(gra_hbm.at[part], gra_ref.at[part], sem.at[1, c]),
-        )
-
-    first = pltpu.make_async_copy(table_hbm, table_ref, sem.at[2, 0])
-    first.start()
-    for c in range(nx // STEP):
-        for copy in copies(c):
-            copy.start()
-    first.wait()
-    table = scalars(table_ref)
+def block_kernel(rows_ref, mat_ref, gra_ref, eps_ref, packed_ref):
+    nx, ny = mat_ref.shape[0], mat_ref.shape[1]
+    table = [jnp.broadcast_to(rows_ref[k : k + 1], (ny, 128)) for k in range(8)]
     lane = lanes((ny, 128))
 
     def one(c, packed):
-        for copy in copies(c):
-            copy.wait()
         for k in range(STEP):
             x = c * STEP + k
             value = lookup(mat_ref[x], table, gra_ref[x])
@@ -116,8 +108,9 @@
 
 
 def joined(parity_ref, even_ref, odd_ref):
-    lane = lanes(even_ref.shape)
-    return jnp.where(((lane >> 1) & 1) == parity_ref[0], odd_ref[...], even_ref[...])
+    lane = lanes(odd_ref.shape)
+    parity = parity_ref[0]
+    return jnp.where(((lane >> 1) & 1) == parity, odd_ref[...], even_ref[1 - parity])
 
 
 def xface_kernel(parity_ref, eps_ref, low_ref, high_ref, even_ref, odd_ref, fwd_ref, bwd_ref):
@@ -182,93 +175,110 @@
     return (gx * fx + recip, gy * fy + recip, gz * fz + recip, gx * fy, gx * fz, gy * fz)
 
 
-CHUNK = 4
-UNROLL = 4
+GROUP = 2
+BEHIND = 3 + 4 // GROUP
 
 
 def inner_kernel(
     parity_ref, eps_ref, low_ref, high_ref, even_ref, odd_ref,
-    out_ref, yb_out, yd_out, zd_out, yi_out,
-    rim, halo, side, box, der, inv, yb, yd, zd, yi, obuf, sem,
+    out_ref, yb, yd, zd, yi, tail,
+    rim, halo, side, box, der, inv, obuf, sem,
 ):
     nx, ny = eps_ref.shape[0], eps_ref.shape[1]
     halo[...] = joined(parity_ref, even_ref, odd_ref)
-    lane = lanes((ny + 8, 128))
+    lane = lanes((8, 128))
     ones = jnp.ones((4, 128), F32)
     for x in range(nx):
         rim[x, 0:2] = low_ref[2 * x : 2 * x + 2]
         rim[x, 2:4] = high_ref[2 * x : 2 * x + 2]
         rim[x, 4:8] = ones
 
-    def turned(c, _):
-        for k in range(UNROLL):
-            x = c * UNROLL + k
-            side[x] = pltpu.roll(halo[...], lax.rem(254 - 4 * x, 128), 1)
-        return 0
-
-    lax.fori_loop(0, nx // UNROLL, turned, 0)
-
-    def along_z(c, _):
-        for k in range(UNROLL):
-            x = c * UNROLL + k
-            v = jnp.concatenate([eps_ref[x], rim[x]], axis=0)
-            for ref, value in zip((box, der, inv), zsums(v, side[x], lane)):
-                put(ref, x, value, ny)
-        return 0
-
-    lax.fori_loop(0, nx // UNROLL, along_z, 0)
-
-    def along_y(x, _):
+    def turned(x):
+        for r in range(0, ny + 8, 8):
+            side[x, r : r + 8] = pltpu.roll(halo[r : r + 8], lax.rem(254 - 4 * x, 128), 1)
+
+    def along_z(x):
+        refs = (box, der, inv)
+        for r in range(0, ny, 8):
+            sums = zsums(eps_ref[x, r : r + 8], side[x, r : r + 8], lane)
+            for ref, value in zip(refs, sums):
+                ref[x, 8 + r : 16 + r] = value
+        for ref, value in zip(refs, zsums(rim[x], side[x, ny : ny + 8], lane)):
+            ref[x, 6:8] = value[0:2]
+            ref[x, 8 + ny : 10 + ny] = value[2:4]
+
+    def along_y(x):
+        for r in range(0, ny, 8):
+            for ref, value in zip((yb, yd, zd, yi), ysums((box, der, inv), x, 8, r)):
+                ref[x, r : r + 8] = value
+
+    def along_x(x, buffer, at):
         for r in range(0, ny, 16):
-            for ref, value in zip((yb, yd, zd, yi), ysums((box, der, inv), x, 16, r)):
-                ref[x, r : r + 16] = value
-        return 0
-
-    lax.fori_loop(0, nx, along_y, 0)
-    for ref, out, wide in ((yb, yb_out, 4), (yd, yd_out, 3), (zd, zd_out, 3), (yi, yi_out, 3)):
-        out[0:wide] = ref[0:wide]
-        out[wide : 2 * wide] = ref[nx - wide : nx]
+            part = slice(r, r + 16)
+            values = result(
+                [yb[x + j, part] for j in (-2, -1, 0, 1, 2)],
+                *[[ref[x + j, part] for j in (-1, 0, 1)] for ref in (yd, zd, yi)],
+            )
+            for n, value in enumerate(values):
+                buffer[n, at, part] = value.astype(jnp.bfloat16)
 
     def copy(c):
+        part = GROUP * c
         return pltpu.make_async_copy(
-            obuf.at[:, pl.ds(c * CHUNK, CHUNK)], out_ref.at[:, pl.ds(2 + c * CHUNK, CHUNK)], sem.at[c]
+            obuf.at[:, pl.ds(part, GROUP)], out_ref.at[:, pl.ds(2 + part, GROUP)], sem.at[c]
         )
 
-    chunks = (nx - 4) // CHUNK
-
-    def along_x(c, _):
-        def one(k, _):
-            at = c * CHUNK + k
-            x = at + 2
-            for r in range(0, ny, 16):
-                part = slice(r, r + 16)
-                values = result(
-                    [yb[x + j, part] for j in (-2, -1, 0, 1, 2)],
-                    *[[ref[x + j, part] for j in (-1, 0, 1)] for ref in (yd, zd, yi)],
-                )
-                for n, value in enumerate(values):
-                    obuf[n, at, part] = value.astype(jnp.bfloat16)
-            return 0
-
-        lax.fori_loop(0, CHUNK, one, 0)
-        copy(c).start()
-        return 0
-
-    lax.fori_loop(0, chunks, along_x, 0)
-
-    def finish(c, _):
+    groups = nx // GROUP
+    last = (nx - 4) // GROUP
+    early = groups + 1 - BEHIND
+    stages = (
+        (turned, 0, groups),
+        (along_z, 1, groups),
+        (along_y, 2, groups),
+        (along_x, BEHIND, last),
+    )
+
+    def run(j, active):
+        for stage, lag in active:
+            for k in range(GROUP):
+                x = (j - lag) * GROUP + k
+                if stage is not along_x:
+                    stage(x)
+                elif along_z in [other for other, _ in active]:
+                    stage(x + 2, obuf, x)
+                else:
+                    stage(x + 2, tail, x - early * GROUP)
+        if active[0][0] is along_x and along_z in [other for other, _ in active]:
+            copy(j - BEHIND).start()
+
+    edges = sorted({lag for _, lag, _ in stages} | {lag + n for _, lag, n in stages})
+    for start, stop in zip(edges, edges[1:]):
+        active = [(stage, lag) for stage, lag, n in stages[::-1] if lag <= start < lag + n]
+
+        def body(j, carry, active=active):
+            run(j, active)
+            return carry
+
+        if active:
+            lax.fori_loop(start, stop, body, 0)
+
+    def finish(c, carry):
         copy(c).wait()
-        return 0
-
-    lax.fori_loop(0, chunks, finish, 0)
+        return carry
+
+    lax.fori_loop(0, early, finish, 0)
 
 
 def outer_kernel(
-    low_ref, high_ref, yb_in, yd_in, zd_in, yi_in, _, out_ref,
+    low_ref, high_ref, yb_in, yd_in, zd_in, yi_in, tail, _, out_ref,
     box, der, inv, yb, yd, zd, yi, obuf, sem,
 ):
     nx, ny = out_ref.shape[1], out_ref.shape[2]
     rows = ny + 8
+    late = pltpu.make_async_copy(
+        tail, out_ref.at[:, pl.ds(nx - 2 - tail.shape[1], tail.shape[1])], sem.at[2]
+    )
+    late.start()
     lane = lanes((rows, 128))
     for k, (ref, s) in enumerate(((low_ref, 0), (low_ref, 1), (high_ref, 0), (high_ref, 1))):
         v = ref[s * rows : (s + 1) * rows]
@@ -284,19 +294,19 @@
                 ref[k, r : r + 16] = value
     for side in range(2):
         for s in range(2):
-            def pick(halo_ref, own_ref, wide, j, part):
+            def pick(halo_ref, own_ref, j, part):
                 x = s + j
                 if side == 0:
                     return halo_ref[2 + x, part] if x < 0 else own_ref[x, part]
                 x = x - 2
-                return halo_ref[2 + x, part] if x >= 0 else own_ref[2 * wide + x, part]
+                return halo_ref[2 + x, part] if x >= 0 else own_ref[nx + x, part]
 
             for r in range(0, ny, 16):
                 part = slice(r, r + 16)
                 values = result(
-                    [pick(yb, yb_in, 4, j, part) for j in (-2, -1, 0, 1, 2)],
+                    [pick(yb, yb_in, j, part) for j in (-2, -1, 0, 1, 2)],
                     *[
-                        [pick(h, o, 3, j, part) for j in (-1, 0, 1)]
+                        [pick(h, o, j, part) for j in (-1, 0, 1)]
                         for h, o in ((yd, yd_in), (zd, zd_in), (yi, yi_in))
                     ],
                 )
@@ -309,6 +319,7 @@
         pltpu.make_async_copy(
             obuf.at[:, pl.ds(2 * side, 2)], out_ref.at[:, pl.ds(side * (nx - 2), 2)], sem.at[side]
         ).wait()
+    late.wait()
 
 
 def cost(us):
@@ -327,44 +338,45 @@
     )
     forward = [(i, (i + 1) % 8) for i in range(8)]
     backward = [(b, a) for a, b in forward]
-    even = [(i, i ^ 1) for i in range(8)]
+    pairs = [[0, 1], [2, 3], [4, 5], [6, 7]]
     odd = [((i + 1) % 8, ((i ^ 1) + 1) % 8) for i in range(8)]
     parity = (lax.axis_index("gz") & 1).reshape(1)
     vmem = pltpu.CompilerParams(vmem_limit_bytes=24 << 20)
 
-    y_fwd, y_bwd = pl.pallas_call(
-        faces_kernel,
+    y_face = shape(2 * nx + 8, nz)
+    y_fwd, y_bwd, mat_near, gra_near, table_rows = pl.pallas_call(
+        face_kernel,
         in_specs=[HBM] * 3,
-        out_specs=[VMEM, VMEM],
-        out_shape=[shape(2 * nx + 8, nz)] * 2,
+        out_specs=[VMEM] * 5,
+        out_shape=[
+            y_face,
+            y_face,
+            shape(nx, ny, nz, dtype=jnp.int32),
+            shape(nx, ny, nz, dtype=jnp.bfloat16),
+            shape(8, nz),
+        ],
         scratch_shapes=[
             pltpu.SMEM((8,), F32),
             *[pltpu.VMEM((nx, 8, nz), jnp.int32)] * 2,
             *[pltpu.VMEM((nx, 16, nz), jnp.bfloat16)] * 2,
-            pltpu.SemaphoreType.DMA((5,)),
+            pltpu.SemaphoreType.DMA((7,)),
         ],
         compiler_params=vmem,
         cost_estimate=cost(1),
-        name="faces",
+        name="face",
     )(eps_table, material, grading)
     y_low = lax.ppermute(y_fwd, "gy", forward)
     y_high = lax.ppermute(y_bwd, "gy", backward)
 
     eps, packed = pl.pallas_call(
         block_kernel,
-        in_specs=[HBM] * 3,
-        out_specs=[VMEM, VMEM],
+        in_specs=[VMEM] * 3,
+        out_specs=[VMEM] * 2,
         out_shape=[shape(nx, ny, nz), shape(ny, nz)],
-        scratch_shapes=[
-            pltpu.SMEM((8,), F32),
-            pltpu.VMEM((nx, ny, nz), jnp.int32),
-            pltpu.VMEM((nx, ny, nz), jnp.bfloat16),
-            pltpu.SemaphoreType.DMA((3, nx // STEP)),
-        ],
         compiler_params=vmem,
         cost_estimate=cost(3),
         name="block",
-    )(eps_table, material, grading)
+    )(table_rows, mat_near, gra_near)
 
     z_face = pl.pallas_call(
         zface_kernel,
@@ -375,8 +387,8 @@
         cost_estimate=cost(0.2),
         name="zface",
     )(packed, y_low, y_high)
-    z_even = lax.ppermute(z_face, "gz", even)
     z_odd = lax.ppermute(z_face, "gz", odd)
+    z_even = lax.all_gather(z_face, "gz", axis=0, axis_index_groups=pairs)
 
     x_fwd, x_bwd = pl.pallas_call(
         xface_kernel,
@@ -391,20 +403,21 @@
     x_high = lax.ppermute(x_bwd, "gx", backward)
 
     full = (nx, ny + 16, nz)
+    late = nx - 4 - (nx // GROUP + 1 - BEHIND) * GROUP
     out, *edges = pl.pallas_call(
         inner_kernel,
         in_specs=[SMEM] + [VMEM] * 5,
-        out_specs=[ANY] + [VMEM] * 4,
-        out_shape=[shape(6, nx, ny, nz, dtype=jnp.bfloat16), shape(8, ny, nz)]
-        + [shape(6, ny, nz)] * 3,
+        out_specs=[ANY] + [VMEM] * 5,
+        out_shape=[shape(6, nx, ny, nz, dtype=jnp.bfloat16)]
+        + [shape(nx, ny, nz)] * 4
+        + [shape(6, late, ny, nz, dtype=jnp.bfloat16)],
         scratch_shapes=[
             pltpu.VMEM((nx, 8, nz), F32),
             pltpu.VMEM((rows, nz), F32),
             pltpu.VMEM((nx, rows, nz), F32),
-            *[pltpu.VMEM(full, F32)] * 3,
-            *[pltpu.VMEM((nx, ny, nz), F32)] * 4,
-            pltpu.VMEM((6, nx - 4, ny, nz), jnp.bfloat16),
-            pltpu.SemaphoreType.DMA(((nx - 4) // CHUNK,)),
+            *[pltpu.VMEM((nx, ny + 16, nz), F32)] * 3,
+            pltpu.VMEM((6, nx - 4 - late, ny, nz), jnp.bfloat16),
+            pltpu.SemaphoreType.DMA(((nx - 4 - late) // GROUP,)),
         ],
         compiler_params=vmem,
         cost_estimate=cost(6),
@@ -413,15 +426,15 @@
 
     return pl.pallas_call(
         outer_kernel,
-        in_specs=[VMEM] * 6 + [ANY],
+        in_specs=[VMEM] * 7 + [ANY],
         out_specs=ANY,
         out_shape=shape(6, nx, ny, nz, dtype=jnp.bfloat16),
-        input_output_aliases={6: 0},
+        input_output_aliases={7: 0},
         scratch_shapes=[
             *[pltpu.VMEM((4, ny + 16, nz), F32)] * 3,
             *[pltpu.VMEM((4, ny, nz), F32)] * 4,
             pltpu.VMEM((6, 4, ny, nz), jnp.bfloat16),
-            pltpu.SemaphoreType.DMA((2,)),
+            pltpu.SemaphoreType.DMA((3,)),
         ],
         compiler_params=vmem,
         cost_estimate=cost(1),

time: 41.2 us -> 38.3 us (0.930); the launches traced: 40.9 us -> 37.6 us
  starting transfers between devices: 29 us -> 26.4 us
  Pallas kernels: 11 us -> 8.67 us
  blocking collectives: 0 us -> 2.16 us
  waiting for transfers between devices: 0.84 us -> 0.23 us
    ppermute x1 -> x0, starting transfers between devices: 3.13 us -> none  [local(): z_even = lax.ppermute(z_face, 'gz', even)]
    all_gather x0 -> x1, blocking collectives: none -> 2.16 us  [local(): z_even = lax.all_gather(z_face, 'gz', axis=0, axis_index_groups=pairs)]
    pallas_call x1, Pallas kernels: 6.36 us -> 4.79 us  [local(): pl.pallas_call(inner_kernel, in_specs=[SMEM] + [VMEM] * 5, out_specs=[ANY...]
    ppermute x1 -> x0, waiting for transfers between devices: 0.83 us -> none  [local(): z_even = lax.ppermute(z_face, 'gz', even)]
    pallas_call x3, Pallas kernels: 4.52 us -> 3.79 us  [the longest x1 1.69 us: local(): pl.pallas_call(face_kernel, in_specs=[HBM] * 3, out_specs=[VMEM] * 5, out...]
    ppermute x1, starting transfers between devices: 5.06 us -> 5.62 us  [local(): z_odd = lax.ppermute(z_face, 'gz', odd)]
  transfers between devices with their start and end apart: 6 -> 5, of which waited for: 1 -> 1; matrix products, arithmetic and copies ran while one was open for 0% -> 0% of each run, Pallas kernels for 20% -> 15%
where the time goes in v3:
time: 38.3 us; the launch traced here: 37.6 us
  starting transfers between devices  26.4 us (69%)
  Pallas kernels  8.67 us (23%)
  blocking collectives  2.16 us (6%)
    ppermute x1, starting transfers between devices, local(): y_high = lax.ppermute(y_bwd, 'gy', backward)  8.59 us
    ppermute x1, starting transfers between devices, local(): z_odd = lax.ppermute(z_face, 'gz', odd)  5.62 us
    ppermute x1, starting transfers between devices, local(): y_low = lax.ppermute(y_fwd, 'gy', forward)  4.82 us
    pallas_call x1, Pallas kernels, local(): pl.pallas_call(inner_kernel, in_specs=[SMEM] + [VMEM] * 5, out_specs=[ANY...  4.79 us
    ppermute x1, starting transfers between devices, local(): x_high = lax.ppermute(x_bwd, 'gx', backward)  4.27 us
    ppermute x1, starting transfers between devices, local(): x_low = lax.ppermute(x_fwd, 'gx', forward)  3.12 us
    all_gather x1, blocking collectives, local(): z_even = lax.all_gather(z_face, 'gz', axis=0, axis_index_groups=pairs)  2.16 us
    pallas_call x1, Pallas kernels, local(): pl.pallas_call(face_kernel, in_specs=[HBM] * 3, out_specs=[VMEM] * 5, out...  1.69 us
  transfers between devices with their start and end apart: 5, of which 1 were waited for; matrix products, arithmetic and copies ran while one was open for 0% of the time, Pallas kernels for 15%

profile of v3, /device:TPU:1, one launch (start us, length us, event | category | flops | bytes accessed | tf_op | source)
XLA Modules:
  0.0 37.6 jit_solution(16973489894476991043)
XLA Ops:
  0.0 1.7 %face.1 = (f32[72,128]{1,0:T(8,128)S(1)}, f32[72,128]{1,0:T(8,128)S(1)}, s32[32,64,128]{2,1,0:T(8,128)S(1)}, bf16[32,64,128]{2,1,0:T(8,128)(2,1)S(1)}, f32[8,128]{1,0:T(8,128)S(1)}) custom-call(f32[8]{0:T(128)} %table_hbm.1, s32[32,64,128]{2,1,0:T(8,128)} %mat_hbm.1, bf16[32,64,128]{2,1,0:T(8,128)(2,1)} %gra_hbm.1), custom_call_target="tpu_custom_call" | custom-call | flops 4000000 | bytes 1000000 | tf_op jit(solution)/shard_map/face/pallas_call | solution.py:347
  1.7 4.8 %collective-permute-start = (f32[72,128]{1,0:T(8,128)S(1)}, f32[72,128]{1,0:T(8,128)S(1)}, u32[]{:S(2)}, u32[]{:S(2)}) collective-permute-start(f32[72,128]{1,0:T(8,128)S(1)} %get-tuple-element.24), channel_id=1, source_target_pairs={{0,8},{8,16},{16,24},{24,32},{32,40},{40,48},{48,56},{56,0},{1,9},... | collective-permute-start | bytes 110600 | tf_op jit(solution)/shard_map/ppermute | solution.py:368
  6.5 8.6 %collective-permute-start.1 = (f32[72,128]{1,0:T(8,128)S(1)}, f32[72,128]{1,0:T(8,128)S(1)}, u32[]{:S(2)}, u32[]{:S(2)}) collective-permute-start(f32[72,128]{1,0:T(8,128)S(1)} %get-tuple-element.25), channel_id=1, source_target_pairs={{8,0},{16,8},{24,16},{32,24},{40,32},{48,40},{56,48},{0,56},{9,1},... | collective-permute-start | bytes 110600 | tf_op jit(solution)/shard_map/ppermute | solution.py:369
  15.1 0.8 %block.1 = (f32[32,64,128]{2,1,0:T(8,128)S(1)}, f32[64,128]{1,0:T(8,128)S(1)}) custom-call(f32[8,128]{1,0:T(8,128)S(1)} %get-tuple-element.20.rows_ref, s32[32,64,128]{2,1,0:T(8,128)S(1)} %get-tuple-element.21.mat_ref, bf16[32,64,128]{2,1,0:T(8,128)(2,1)S(1)} %get-tuple-element.22.gra_ref), custom_call_target="tpu_custom_call" | custom-call | flops 12000000 | bytes 3000000 | tf_op jit(solution)/shard_map/block/pallas_call | solution.py:371
  15.9 0.0 collective-permute-done.low_ref
  15.9 0.2 collective-permute-done.1.high_ref
  16.2 5.6 %collective-permute-start.2 = (f32[72,128]{1,0:T(8,128)S(1)}, f32[72,128]{1,0:T(8,128)S(1)}, u32[]{:S(2)}, u32[]{:S(2)}) collective-permute-start(f32[72,128]{1,0:T(8,128)S(1)} %zface.1), channel_id=1, source_target_pairs={{1,2},{2,1},{3,4},{4,3},{5,6},{6,5},{7,0},{0,7},{9,10},{10,9},{11,... | collective-permute-start | bytes 110600 | tf_op jit(solution)/shard_map/ppermute | solution.py:390
  21.8 2.2 %all-gather = f32[144,128]{1,0:T(8,128)S(1)} all-gather(f32[72,128]{1,0:T(8,128)S(1)} %zface.1), channel_id=2, replica_groups={{0,1},{2,3},{4,5},{6,7},{8,9},{10,11},{12,13},{14,15},{16,17},{18,19},{..., dimensions={0}, use_global_device_ids=true | all-gather | bytes 110592 | tf_op jit(solution)/shard_map/all_gather | solution.py:391
  24.0 0.0 collective-permute-done.2.odd_ref
  24.0 0.1 xface.1
  24.0 3.1 %collective-permute-start.3 = (f32[152,128]{1,0:T(8,128)S(1)}, f32[152,128]{1,0:T(8,128)S(1)}, u32[]{:S(2)}, u32[]{:S(2)}) collective-permute-start(f32[152,128]{1,0:T(8,128)S(1)} %get-tuple-element.27), channel_id=1, source_target_pairs={{0,64},{64,128},{128,192},{192,256},{256,320},{320,384},{384,448},... | collective-permute-start | bytes 233480 | tf_op jit(solution)/shard_map/ppermute | solution.py:402
  27.2 4.3 %collective-permute-start.4 = (f32[152,128]{1,0:T(8,128)S(1)}, f32[152,128]{1,0:T(8,128)S(1)}, u32[]{:S(2)}, u32[]{:S(2)}) collective-permute-start(f32[152,128]{1,0:T(8,128)S(1)} %get-tuple-element.28), channel_id=1, source_target_pairs={{64,0},{128,64},{192,128},{256,192},{320,256},{384,320},{448,384},... | collective-permute-start | bytes 233480 | tf_op jit(solution)/shard_map/ppermute | solution.py:403
  31.5 4.8 %inner.1 = (bf16[6,32,64,128]{3,2,1,0:T(8,128)(2,1)}, f32[32,64,128]{2,1,0:T(8,128)S(1)}, f32[32,64,128]{2,1,0:T(8,128)S(1)}, f32[32,64,128]{2,1,0:T(8,128)S(1)}...) custom-call(s32[1]{0:T(128)} %bitcast.parity_ref, f32[32,64,128]{2,1,0:T(8,128)S(1)} %get-tuple-element.23.eps_ref, ...), custom_call_target="tpu_custom_call" | custom-call | flops 24000000 | bytes 6000000 | tf_op jit(solution)/shard_map/inner/pallas_call | solution.py:407
  36.2 0.0 collective-permute-done.3.low_ref
  36.3 0.0 collective-permute-done.4.high_ref
  36.3 1.3 %outer.1 = bf16[6,32,64,128]{3,2,1,0:T(8,128)(2,1)} custom-call(f32[152,128]{1,0:T(8,128)S(1)} %collective-permute-done.3.low_ref, f32[152,128]{1,0:T(8,128)S(1)} %collective-permute-done.4.high_ref, f32[32,64,128]{2,1,0:T(8,128)S(1)} %get-tuple-element.29.yb_in, f32[32,64,128]{2,1,0:T(8,128)S(1)} %get-tuple-element.30.yd_in, ...), custom_call_target="tpu_custom_call", output_to_operand_aliasing={{}: (7, {})} | custom-call | flops 4000000 | bytes 1000000 | tf_op jit(solution)/shard_map/outer/pallas_call | solution.py:427
  (1 shorter events, 0.0 us)
Async XLA Ops:
  1.7 14.2 %collective-permute-start = (f32[72,128]{1,0:T(8,128)S(1)}, f32[72,128]{1,0:T(8,128)S(1)}, u32[]{:S(2)}, u32[]{:S(2)}) collective-permute-start(f32[72,128]{1,0:T(8,128)S(1)} %get-tuple-element.24), channel_id=1, source_target_pairs={{0,8},{8,16},{16,24},{24,32},{32,40},{40,48},{48,56},{56,0},{1,9},... | collective-permute-start | bytes 110600 | tf_op jit(solution)/shard_map/ppermute | solution.py:368
  6.5 9.6 %collective-permute-start.1 = (f32[72,128]{1,0:T(8,128)S(1)}, f32[72,128]{1,0:T(8,128)S(1)}, u32[]{:S(2)}, u32[]{:S(2)}) collective-permute-start(f32[72,128]{1,0:T(8,128)S(1)} %get-tuple-element.25), channel_id=1, source_target_pairs={{8,0},{16,8},{24,16},{32,24},{40,32},{48,40},{56,48},{0,56},{9,1},... | collective-permute-start | bytes 110600 | tf_op jit(solution)/shard_map/ppermute | solution.py:369
  16.2 7.8 %collective-permute-start.2 = (f32[72,128]{1,0:T(8,128)S(1)}, f32[72,128]{1,0:T(8,128)S(1)}, u32[]{:S(2)}, u32[]{:S(2)}) collective-permute-start(f32[72,128]{1,0:T(8,128)S(1)} %zface.1), channel_id=1, source_target_pairs={{1,2},{2,1},{3,4},{4,3},{5,6},{6,5},{7,0},{0,7},{9,10},{10,9},{11,... | collective-permute-start | bytes 110600 | tf_op jit(solution)/shard_map/ppermute | solution.py:390
  24.0 12.2 %collective-permute-start.3 = (f32[152,128]{1,0:T(8,128)S(1)}, f32[152,128]{1,0:T(8,128)S(1)}, u32[]{:S(2)}, u32[]{:S(2)}) collective-permute-start(f32[152,128]{1,0:T(8,128)S(1)} %get-tuple-element.27), channel_id=1, source_target_pairs={{0,64},{64,128},{128,192},{192,256},{256,320},{320,384},{384,448},... | collective-permute-start | bytes 233480 | tf_op jit(solution)/shard_map/ppermute | solution.py:402
  27.2 9.1 %collective-permute-start.4 = (f32[152,128]{1,0:T(8,128)S(1)}, f32[152,128]{1,0:T(8,128)S(1)}, u32[]{:S(2)}, u32[]{:S(2)}) collective-permute-start(f32[152,128]{1,0:T(8,128)S(1)} %get-tuple-element.28), channel_id=1, source_target_pairs={{64,0},{128,64},{192,128},{256,192},{320,256},{384,320},{448,384},... | collective-permute-start | bytes 233480 | tf_op jit(solution)/shard_map/ppermute | solution.py:403

commit v4 on v3

--- a/solution.py
+++ b/solution.py
@@ -35,36 +35,34 @@
 
 
 def face_kernel(
-    table_hbm, mat_hbm, gra_hbm, fwd_ref, bwd_ref, mat_ref, gra_ref, rows_ref,
-    table_ref, mat_low, mat_high, gra_low, gra_high, sem,
+    table_hbm, mat_hbm, gra_hbm, fwd_ref, bwd_ref, mat_ref, gra_ref, rows_ref, table_ref, sem
 ):
     nx, ny = mat_hbm.shape[0], mat_hbm.shape[1]
-    copies = [
-        pltpu.make_async_copy(src, dst, sem.at[k])
-        for k, (src, dst) in enumerate(
-            (
-                (table_hbm, table_ref),
-                (mat_hbm.at[:, 0:8], mat_low),
-                (gra_hbm.at[:, 0:16], gra_low),
-                (mat_hbm.at[:, ny - 8 : ny], mat_high),
-                (gra_hbm.at[:, ny - 16 : ny], gra_high),
-                (mat_hbm, mat_ref),
-                (gra_hbm, gra_ref),
-            )
-        )
-    ]
-    for copy in copies:
-        copy.start()
-    for copy in copies[:5]:
-        copy.wait()
+    begin = pltpu.make_async_copy(table_hbm, table_ref, sem.at[2, 0])
+    begin.start()
+    copies = []
+    for c in range(nx // STEP):
+        part = slice(c * STEP, (c + 1) * STEP)
+        copies.append(
+            [
+                pltpu.make_async_copy(src.at[part], dst.at[part], sem.at[k, c])
+                for k, (src, dst) in enumerate(((mat_hbm, mat_ref), (gra_hbm, gra_ref)))
+            ]
+        )
+        for copy in copies[c]:
+            copy.start()
+    begin.wait()
     table = scalars(table_ref)
     for k in range(8):
         rows_ref[k : k + 1] = jnp.full((1, 128), table[k], F32)
     lane = lanes((8, 128))
     packed = [jnp.zeros((8, 128), F32)] * 2
     for x in range(nx):
-        low = lookup(mat_low[x], table, gra_low[x, 0:8])
-        high = lookup(mat_high[x], table, gra_high[x, 8:16])
+        if x % STEP == 0:
+            for copy in copies[x // STEP]:
+                copy.wait()
+        low = lookup(mat_ref[x, 0:8], table, gra_ref[x, 0:8])
+        high = lookup(mat_ref[x, ny - 8 : ny], table, gra_ref[x, ny - 8 : ny])
         bwd_ref[2 * x : 2 * x + 2] = low[0:2]
         fwd_ref[2 * x : 2 * x + 2] = high[6:8]
         turn = (4 * x + 2) % 128
@@ -74,8 +72,6 @@
         ]
     finish_face(bwd_ref, packed[0][0:2], nx)
     finish_face(fwd_ref, packed[1][6:8], nx)
-    for copy in copies[5:]:
-        copy.wait()
 
 
 STEP = 8
@@ -144,6 +140,25 @@
     return v + left + right, (right + right2) - (left + left2), inv + inv_left + inv_right
 
 
+def inverse_zsum(v, h, lane):
+    inv, inv_h = 1.0 / v, 1.0 / h
+    inv_left = pltpu.roll(jnp.where(lane == 127, inv_h, inv), 1, 1)
+    inv_right = pltpu.roll(jnp.where(lane == 0, inv_h, inv), 127, 1)
+    return inv + inv_left + inv_right
+
+
+def tap_matrix():
+    shape = (512, 256)
+    row = lax.broadcasted_iota(jnp.int32, shape, 0) & 255
+    column = lax.broadcasted_iota(jnp.int32, shape, 1)
+    place = jnp.where(row < 128, row, jnp.where(row >= 192, row - 256, row))
+    away = place - (column & 127)
+    box = jnp.where(jnp.abs(away) <= 1, 1.0, 0.0)
+    outer = jnp.where((jnp.abs(away) == 1) | (jnp.abs(away) == 2), 1.0, 0.0)
+    der = jnp.where(away > 0, outer, -outer)
+    return jnp.where(column < 128, box, der).astype(jnp.bfloat16)
+
+
 def put(ref, index, value, ny):
     ref[index, 8 : 8 + ny] = value[0:ny]
     ref[index, 6:8] = value[ny : ny + 2]
@@ -175,17 +190,18 @@
     return (gx * fx + recip, gy * fy + recip, gz * fz + recip, gx * fy, gx * fz, gy * fz)
 
 
-GROUP = 2
+GROUP = 4
 BEHIND = 3 + 4 // GROUP
 
 
 def inner_kernel(
     parity_ref, eps_ref, low_ref, high_ref, even_ref, odd_ref,
     out_ref, yb, yd, zd, yi, tail,
-    rim, halo, side, box, der, inv, obuf, sem,
+    rim, halo, side, taps, box, der, inv, obuf, sem,
 ):
     nx, ny = eps_ref.shape[0], eps_ref.shape[1]
     halo[...] = joined(parity_ref, even_ref, odd_ref)
+    taps[...] = tap_matrix()
     lane = lanes((8, 128))
     ones = jnp.ones((4, 128), F32)
     for x in range(nx):
@@ -197,15 +213,32 @@
         for r in range(0, ny + 8, 8):
             side[x, r : r + 8] = pltpu.roll(halo[r : r + 8], lax.rem(254 - 4 * x, 128), 1)
 
-    def along_z(x):
-        refs = (box, der, inv)
-        for r in range(0, ny, 8):
-            sums = zsums(eps_ref[x, r : r + 8], side[x, r : r + 8], lane)
-            for ref, value in zip(refs, sums):
-                ref[x, 8 + r : 16 + r] = value
-        for ref, value in zip(refs, zsums(rim[x], side[x, ny : ny + 8], lane)):
-            ref[x, 6:8] = value[0:2]
-            ref[x, 8 + ny : 10 + ny] = value[2:4]
+    def along_z(c):
+        slices = range(GROUP)
+        for k in slices:
+            x = c * GROUP + k
+            for r in range(0, ny, 8):
+                value = inverse_zsum(eps_ref[x, r : r + 8], side[x, r : r + 8], lane)
+                inv[x, 8 + r : 16 + r] = value
+            value = inverse_zsum(rim[x], side[x, ny : ny + 8], lane)
+            inv[x, 6:8] = value[0:2]
+            inv[x, 8 + ny : 10 + ny] = value[2:4]
+        own = jnp.concatenate(
+            [part for k in slices for part in (eps_ref[c * GROUP + k], rim[c * GROUP + k])], axis=0
+        )
+        near = jnp.concatenate([side[c * GROUP + k] for k in slices], axis=0)
+        values = jnp.concatenate([own, near], axis=1)
+        coarse = values.astype(jnp.bfloat16)
+        fine = (values - coarse.astype(F32)).astype(jnp.bfloat16)
+        sums = jnp.dot(
+            jnp.concatenate([coarse, fine], axis=1), taps[...], preferred_element_type=F32
+        )
+        for ref, part in ((box, sums[:, 0:128]), (der, sums[:, 128:256])):
+            for k in slices:
+                x, at = c * GROUP + k, k * (ny + 8)
+                ref[x, 8 : 8 + ny] = part[at : at + ny]
+                ref[x, 6:8] = part[at + ny : at + ny + 2]
+                ref[x, 8 + ny : 10 + ny] = part[at + ny + 2 : at + ny + 4]
 
     def along_y(x):
         for r in range(0, ny, 8):
@@ -240,6 +273,9 @@
 
     def run(j, active):
         for stage, lag in active:
+            if stage is along_z:
+                stage(j - lag)
+                continue
             for k in range(GROUP):
                 x = (j - lag) * GROUP + k
                 if stage is not along_x:
@@ -276,9 +312,16 @@
     nx, ny = out_ref.shape[1], out_ref.shape[2]
     rows = ny + 8
     late = pltpu.make_async_copy(
-        tail, out_ref.at[:, pl.ds(nx - 2 - tail.shape[1], tail.shape[1])], sem.at[2]
+        tail, out_ref.at[:, pl.ds(nx - 2 - tail.shape[1], tail.shape[1])], sem.at[4]
     )
     late.start()
+
+    def finish(k):
+        x = k if k < 2 else nx - 4 + k
+        return pltpu.make_async_copy(
+            obuf.at[:, pl.ds(k, 1)], out_ref.at[:, pl.ds(x, 1)], sem.at[k]
+        )
+
     lane = lanes((rows, 128))
     for k, (ref, s) in enumerate(((low_ref, 0), (low_ref, 1), (high_ref, 0), (high_ref, 1))):
         v = ref[s * rows : (s + 1) * rows]
@@ -312,13 +355,9 @@
                 )
                 for n, value in enumerate(values):
                     obuf[n, 2 * side + s, part] = value.astype(jnp.bfloat16)
-        pltpu.make_async_copy(
-            obuf.at[:, pl.ds(2 * side, 2)], out_ref.at[:, pl.ds(side * (nx - 2), 2)], sem.at[side]
-        ).start()
-    for side in range(2):
-        pltpu.make_async_copy(
-            obuf.at[:, pl.ds(2 * side, 2)], out_ref.at[:, pl.ds(side * (nx - 2), 2)], sem.at[side]
-        ).wait()
+            finish(2 * side + s).start()
+    for k in range(4):
+        finish(k).wait()
     late.wait()
 
 
@@ -357,9 +396,7 @@
         ],
         scratch_shapes=[
             pltpu.SMEM((8,), F32),
-            *[pltpu.VMEM((nx, 8, nz), jnp.int32)] * 2,
-            *[pltpu.VMEM((nx, 16, nz), jnp.bfloat16)] * 2,
-            pltpu.SemaphoreType.DMA((7,)),
+            pltpu.SemaphoreType.DMA((3, nx // STEP)),
         ],
         compiler_params=vmem,
         cost_estimate=cost(1),
@@ -415,6 +452,7 @@
             pltpu.VMEM((nx, 8, nz), F32),
             pltpu.VMEM((rows, nz), F32),
             pltpu.VMEM((nx, rows, nz), F32),
+            pltpu.VMEM((512, 256), jnp.bfloat16),
             *[pltpu.VMEM((nx, ny + 16, nz), F32)] * 3,
             pltpu.VMEM((6, nx - 4 - late, ny, nz), jnp.bfloat16),
             pltpu.SemaphoreType.DMA(((nx - 4 - late) // GROUP,)),
@@ -434,7 +472,7 @@
             *[pltpu.VMEM((4, ny + 16, nz), F32)] * 3,
             *[pltpu.VMEM((4, ny, nz), F32)] * 4,
             pltpu.VMEM((6, 4, ny, nz), jnp.bfloat16),
-            pltpu.SemaphoreType.DMA((3,)),
+            pltpu.SemaphoreType.DMA((5,)),
         ],
         compiler_params=vmem,
         cost_estimate=cost(1),

time: 38.3 us -> 37.9 us (0.990)
  Pallas kernels: 8.67 us -> 8.28 us
  transfers between devices with their start and end apart: 5 -> 5, of which waited for: 1 -> 1; matrix products, arithmetic and copies ran while one was open for 0% -> 0% of each run, Pallas kernels for 15% -> 14%
where the time goes in v4:
time: 37.9 us; the launch traced here: 37.2 us
  starting transfers between devices  26.4 us (70%)
  Pallas kernels  8.28 us (22%)
  blocking collectives  2.16 us (6%)
    ppermute x1, starting transfers between devices, local(): y_high = lax.ppermute(y_bwd, 'gy', backward)  8.59 us
    ppermute x1, starting transfers between devices, local(): z_odd = lax.ppermute(z_face, 'gz', odd)  5.62 us
    ppermute x1, starting transfers between devices, local(): y_low = lax.ppermute(y_fwd, 'gy', forward)  4.82 us
    pallas_call x1, Pallas kernels, local(): pl.pallas_call(inner_kernel, in_specs=[SMEM] + [VMEM] * 5, out_specs=[ANY...  4.54 us
    ppermute x1, starting transfers between devices, local(): x_high = lax.ppermute(x_bwd, 'gx', backward)  4.27 us
    ppermute x1, starting transfers between devices, local(): x_low = lax.ppermute(x_fwd, 'gx', forward)  3.12 us
    all_gather x1, blocking collectives, local(): z_even = lax.all_gather(z_face, 'gz', axis=0, axis_index_groups=pairs)  2.16 us
    pallas_call x1, Pallas kernels, local(): pl.pallas_call(face_kernel, in_specs=[HBM] * 3, out_specs=[VMEM] * 5, out...  1.57 us
  transfers between devices with their start and end apart: 5, of which 1 were waited for; matrix products, arithmetic and copies ran while one was open for 0% of the time, Pallas kernels for 14%

profile of v4, /device:TPU:1, one launch (start us, length us, event | category | flops | bytes accessed | tf_op | source)
XLA Modules:
  0.0 37.2 jit_solution(11001647472183944574)
XLA Ops:
  0.0 1.6 %face.1 = (f32[72,128]{1,0:T(8,128)S(1)}, f32[72,128]{1,0:T(8,128)S(1)}, s32[32,64,128]{2,1,0:T(8,128)S(1)}, bf16[32,64,128]{2,1,0:T(8,128)(2,1)S(1)}, f32[8,128]{1,0:T(8,128)S(1)}) custom-call(f32[8]{0:T(128)} %table_hbm.1, s32[32,64,128]{2,1,0:T(8,128)} %mat_hbm.1, bf16[32,64,128]{2,1,0:T(8,128)(2,1)} %gra_hbm.1), custom_call_target="tpu_custom_call" | custom-call | flops 4000000 | bytes 1000000 | tf_op jit(solution)/shard_map/face/pallas_call | solution.py:386
  1.6 4.8 %collective-permute-start = (f32[72,128]{1,0:T(8,128)S(1)}, f32[72,128]{1,0:T(8,128)S(1)}, u32[]{:S(2)}, u32[]{:S(2)}) collective-permute-start(f32[72,128]{1,0:T(8,128)S(1)} %get-tuple-element.24), channel_id=1, source_target_pairs={{0,8},{8,16},{16,24},{24,32},{32,40},{40,48},{48,56},{56,0},{1,9},... | collective-permute-start | bytes 110600 | tf_op jit(solution)/shard_map/ppermute | solution.py:405
  6.4 8.6 %collective-permute-start.1 = (f32[72,128]{1,0:T(8,128)S(1)}, f32[72,128]{1,0:T(8,128)S(1)}, u32[]{:S(2)}, u32[]{:S(2)}) collective-permute-start(f32[72,128]{1,0:T(8,128)S(1)} %get-tuple-element.25), channel_id=1, source_target_pairs={{8,0},{16,8},{24,16},{32,24},{40,32},{48,40},{56,48},{0,56},{9,1},... | collective-permute-start | bytes 110600 | tf_op jit(solution)/shard_map/ppermute | solution.py:406
  15.0 0.8 %block.1 = (f32[32,64,128]{2,1,0:T(8,128)S(1)}, f32[64,128]{1,0:T(8,128)S(1)}) custom-call(f32[8,128]{1,0:T(8,128)S(1)} %get-tuple-element.20.rows_ref, s32[32,64,128]{2,1,0:T(8,128)S(1)} %get-tuple-element.21.mat_ref, bf16[32,64,128]{2,1,0:T(8,128)(2,1)S(1)} %get-tuple-element.22.gra_ref), custom_call_target="tpu_custom_call" | custom-call | flops 12000000 | bytes 3000000 | tf_op jit(solution)/shard_map/block/pallas_call | solution.py:408
  15.8 0.0 collective-permute-done.low_ref
  15.8 0.2 collective-permute-done.1.high_ref
  16.0 5.6 %collective-permute-start.2 = (f32[72,128]{1,0:T(8,128)S(1)}, f32[72,128]{1,0:T(8,128)S(1)}, u32[]{:S(2)}, u32[]{:S(2)}) collective-permute-start(f32[72,128]{1,0:T(8,128)S(1)} %zface.1), channel_id=1, source_target_pairs={{1,2},{2,1},{3,4},{4,3},{5,6},{6,5},{7,0},{0,7},{9,10},{10,9},{11,... | collective-permute-start | bytes 110600 | tf_op jit(solution)/shard_map/ppermute | solution.py:427
  21.7 2.2 %all-gather = f32[144,128]{1,0:T(8,128)S(1)} all-gather(f32[72,128]{1,0:T(8,128)S(1)} %zface.1), channel_id=2, replica_groups={{0,1},{2,3},{4,5},{6,7},{8,9},{10,11},{12,13},{14,15},{16,17},{18,19},{..., dimensions={0}, use_global_device_ids=true | all-gather | bytes 110592 | tf_op jit(solution)/shard_map/all_gather | solution.py:428
  23.8 0.0 collective-permute-done.2.odd_ref
  23.8 0.1 xface.1
  23.9 3.1 %collective-permute-start.3 = (f32[152,128]{1,0:T(8,128)S(1)}, f32[152,128]{1,0:T(8,128)S(1)}, u32[]{:S(2)}, u32[]{:S(2)}) collective-permute-start(f32[152,128]{1,0:T(8,128)S(1)} %get-tuple-element.27), channel_id=1, source_target_pairs={{0,64},{64,128},{128,192},{192,256},{256,320},{320,384},{384,448},... | collective-permute-start | bytes 233480 | tf_op jit(solution)/shard_map/ppermute | solution.py:439
  27.1 4.3 %collective-permute-start.4 = (f32[152,128]{1,0:T(8,128)S(1)}, f32[152,128]{1,0:T(8,128)S(1)}, u32[]{:S(2)}, u32[]{:S(2)}) collective-permute-start(f32[152,128]{1,0:T(8,128)S(1)} %get-tuple-element.28), channel_id=1, source_target_pairs={{64,0},{128,64},{192,128},{256,192},{320,256},{384,320},{448,384},... | collective-permute-start | bytes 233480 | tf_op jit(solution)/shard_map/ppermute | solution.py:440
  31.3 4.5 %inner.1 = (bf16[6,32,64,128]{3,2,1,0:T(8,128)(2,1)}, f32[32,64,128]{2,1,0:T(8,128)S(1)}, f32[32,64,128]{2,1,0:T(8,128)S(1)}, f32[32,64,128]{2,1,0:T(8,128)S(1)}...) custom-call(s32[1]{0:T(128)} %bitcast.parity_ref, f32[32,64,128]{2,1,0:T(8,128)S(1)} %get-tuple-element.23.eps_ref, ...), custom_call_target="tpu_custom_call" | custom-call | flops 24000000 | bytes 6000000 | tf_op jit(solution)/shard_map/inner/pallas_call | solution.py:444
  35.9 0.0 collective-permute-done.3.low_ref
  35.9 0.0 collective-permute-done.4.high_ref
  35.9 1.3 %outer.1 = bf16[6,32,64,128]{3,2,1,0:T(8,128)(2,1)} custom-call(f32[152,128]{1,0:T(8,128)S(1)} %collective-permute-done.3.low_ref, f32[152,128]{1,0:T(8,128)S(1)} %collective-permute-done.4.high_ref, f32[32,64,128]{2,1,0:T(8,128)S(1)} %get-tuple-element.29.yb_in, f32[32,64,128]{2,1,0:T(8,128)S(1)} %get-tuple-element.30.yd_in, ...), custom_call_target="tpu_custom_call", output_to_operand_aliasing={{}: (7, {})} | custom-call | flops 4000000 | bytes 1000000 | tf_op jit(solution)/shard_map/outer/pallas_call | solution.py:465
  (1 shorter events, 0.0 us)
Async XLA Ops:
  1.6 14.2 %collective-permute-start = (f32[72,128]{1,0:T(8,128)S(1)}, f32[72,128]{1,0:T(8,128)S(1)}, u32[]{:S(2)}, u32[]{:S(2)}) collective-permute-start(f32[72,128]{1,0:T(8,128)S(1)} %get-tuple-element.24), channel_id=1, source_target_pairs={{0,8},{8,16},{16,24},{24,32},{32,40},{40,48},{48,56},{56,0},{1,9},... | collective-permute-start | bytes 110600 | tf_op jit(solution)/shard_map/ppermute | solution.py:405
  6.4 9.6 %collective-permute-start.1 = (f32[72,128]{1,0:T(8,128)S(1)}, f32[72,128]{1,0:T(8,128)S(1)}, u32[]{:S(2)}, u32[]{:S(2)}) collective-permute-start(f32[72,128]{1,0:T(8,128)S(1)} %get-tuple-element.25), channel_id=1, source_target_pairs={{8,0},{16,8},{24,16},{32,24},{40,32},{48,40},{56,48},{0,56},{9,1},... | collective-permute-start | bytes 110600 | tf_op jit(solution)/shard_map/ppermute | solution.py:406
  16.0 7.8 %collective-permute-start.2 = (f32[72,128]{1,0:T(8,128)S(1)}, f32[72,128]{1,0:T(8,128)S(1)}, u32[]{:S(2)}, u32[]{:S(2)}) collective-permute-start(f32[72,128]{1,0:T(8,128)S(1)} %zface.1), channel_id=1, source_target_pairs={{1,2},{2,1},{3,4},{4,3},{5,6},{6,5},{7,0},{0,7},{9,10},{10,9},{11,... | collective-permute-start | bytes 110600 | tf_op jit(solution)/shard_map/ppermute | solution.py:427
  23.9 12.0 %collective-permute-start.3 = (f32[152,128]{1,0:T(8,128)S(1)}, f32[152,128]{1,0:T(8,128)S(1)}, u32[]{:S(2)}, u32[]{:S(2)}) collective-permute-start(f32[152,128]{1,0:T(8,128)S(1)} %get-tuple-element.27), channel_id=1, source_target_pairs={{0,64},{64,128},{128,192},{192,256},{256,320},{320,384},{384,448},... | collective-permute-start | bytes 233480 | tf_op jit(solution)/shard_map/ppermute | solution.py:439
  27.1 8.8 %collective-permute-start.4 = (f32[152,128]{1,0:T(8,128)S(1)}, f32[152,128]{1,0:T(8,128)S(1)}, u32[]{:S(2)}, u32[]{:S(2)}) collective-permute-start(f32[152,128]{1,0:T(8,128)S(1)} %get-tuple-element.28), channel_id=1, source_target_pairs={{64,0},{128,64},{192,128},{256,192},{320,256},{384,320},{448,384},... | collective-permute-start | bytes 233480 | tf_op jit(solution)/shard_map/ppermute | solution.py:440

commit v5 on v4

--- a/solution.py
+++ b/solution.py
@@ -192,6 +192,7 @@
 
 GROUP = 4
 BEHIND = 3 + 4 // GROUP
+EARLY = 3
 
 
 def inner_kernel(
@@ -263,7 +264,7 @@
 
     groups = nx // GROUP
     last = (nx - 4) // GROUP
-    early = groups + 1 - BEHIND
+    early = EARLY
     stages = (
         (turned, 0, groups),
         (along_z, 1, groups),
@@ -271,7 +272,7 @@
         (along_x, BEHIND, last),
     )
 
-    def run(j, active):
+    def run(j, active, soon):
         for stage, lag in active:
             if stage is along_z:
                 stage(j - lag)
@@ -280,19 +281,21 @@
                 x = (j - lag) * GROUP + k
                 if stage is not along_x:
                     stage(x)
-                elif along_z in [other for other, _ in active]:
+                elif soon:
                     stage(x + 2, obuf, x)
                 else:
                     stage(x + 2, tail, x - early * GROUP)
-        if active[0][0] is along_x and along_z in [other for other, _ in active]:
+        if active[0][0] is along_x and soon:
             copy(j - BEHIND).start()
 
-    edges = sorted({lag for _, lag, _ in stages} | {lag + n for _, lag, n in stages})
+    edges = sorted(
+        {lag for _, lag, _ in stages} | {lag + n for _, lag, n in stages} | {BEHIND + early}
+    )
     for start, stop in zip(edges, edges[1:]):
         active = [(stage, lag) for stage, lag, n in stages[::-1] if lag <= start < lag + n]
 
-        def body(j, carry, active=active):
-            run(j, active)
+        def body(j, carry, active=active, soon=start < BEHIND + early):
+            run(j, active, soon)
             return carry
 
         if active:
@@ -440,7 +443,7 @@
     x_high = lax.ppermute(x_bwd, "gx", backward)
 
     full = (nx, ny + 16, nz)
-    late = nx - 4 - (nx // GROUP + 1 - BEHIND) * GROUP
+    late = nx - 4 - EARLY * GROUP
     out, *edges = pl.pallas_call(
         inner_kernel,
         in_specs=[SMEM] + [VMEM] * 5,

time: 37.9 us -> 37.4 us (0.987)
  the two profiles are of different devices: /device:TPU:1 before, /device:TPU:6 now
where the time goes in v5:
time: 37.4 us; the launch traced here: 37.1 us
  starting transfers between devices  23.4 us (63%)
  Pallas kernels  7.55 us (20%)
  waiting for transfers between devices  4.17 us (11%)
  blocking collectives  1.86 us (5%)
    ppermute x1, starting transfers between devices, local(): y_high = lax.ppermute(y_bwd, 'gy', backward)  8.59 us
    ppermute x1, starting transfers between devices, local(): z_odd = lax.ppermute(z_face, 'gz', odd)  4.74 us
    ppermute x1, starting transfers between devices, local(): y_low = lax.ppermute(y_fwd, 'gy', forward)  4.28 us
    ppermute x1, starting transfers between devices, local(): x_low = lax.ppermute(x_fwd, 'gx', forward)  3.65 us
    pallas_call x1, Pallas kernels, local(): pl.pallas_call(inner_kernel, in_specs=[SMEM] + [VMEM] * 5, out_specs=[ANY...  3.61 us
    ppermute x1, waiting for transfers between devices, local(): x_high = lax.ppermute(x_bwd, 'gx', backward)  2.58 us
    ppermute x1, starting transfers between devices, local(): x_high = lax.ppermute(x_bwd, 'gx', backward)  2.19 us
    all_gather x1, blocking collectives, local(): z_even = lax.all_gather(z_face, 'gz', axis=0, axis_index_groups=pairs)  1.86 us
  transfers between devices with their start and end apart: 5, of which 3 were waited for; matrix products, arithmetic and copies ran while one was open for 0% of the time, Pallas kernels for 12%

profile of v5, /device:TPU:6, one launch (start us, length us, event | category | flops | bytes accessed | tf_op | source)
XLA Modules:
  0.0 37.1 jit_solution(3373535578162446094)
XLA Ops:
  0.0 1.6 %face.1 = (f32[72,128]{1,0:T(8,128)S(1)}, f32[72,128]{1,0:T(8,128)S(1)}, s32[32,64,128]{2,1,0:T(8,128)S(1)}, bf16[32,64,128]{2,1,0:T(8,128)(2,1)S(1)}, f32[8,128]{1,0:T(8,128)S(1)}) custom-call(f32[8]{0:T(128)} %table_hbm.1, s32[32,64,128]{2,1,0:T(8,128)} %mat_hbm.1, bf16[32,64,128]{2,1,0:T(8,128)(2,1)} %gra_hbm.1), custom_call_target="tpu_custom_call" | custom-call | flops 4000000 | bytes 1000000 | tf_op jit(solution)/shard_map/face/pallas_call | solution.py:389
  1.6 4.3 %collective-permute-start = (f32[72,128]{1,0:T(8,128)S(1)}, f32[72,128]{1,0:T(8,128)S(1)}, u32[]{:S(2)}, u32[]{:S(2)}) collective-permute-start(f32[72,128]{1,0:T(8,128)S(1)} %get-tuple-element.24), channel_id=1, source_target_pairs={{0,8},{8,16},{16,24},{24,32},{32,40},{40,48},{48,56},{56,0},{1,9},... | collective-permute-start | bytes 110600 | tf_op jit(solution)/shard_map/ppermute | solution.py:408
  5.9 8.6 %collective-permute-start.1 = (f32[72,128]{1,0:T(8,128)S(1)}, f32[72,128]{1,0:T(8,128)S(1)}, u32[]{:S(2)}, u32[]{:S(2)}) collective-permute-start(f32[72,128]{1,0:T(8,128)S(1)} %get-tuple-element.25), channel_id=1, source_target_pairs={{8,0},{16,8},{24,16},{32,24},{40,32},{48,40},{56,48},{0,56},{9,1},... | collective-permute-start | bytes 110600 | tf_op jit(solution)/shard_map/ppermute | solution.py:409
  14.5 0.8 %block.1 = (f32[32,64,128]{2,1,0:T(8,128)S(1)}, f32[64,128]{1,0:T(8,128)S(1)}) custom-call(f32[8,128]{1,0:T(8,128)S(1)} %get-tuple-element.20.rows_ref, s32[32,64,128]{2,1,0:T(8,128)S(1)} %get-tuple-element.21.mat_ref, bf16[32,64,128]{2,1,0:T(8,128)(2,1)S(1)} %get-tuple-element.22.gra_ref), custom_call_target="tpu_custom_call" | custom-call | flops 12000000 | bytes 3000000 | tf_op jit(solution)/shard_map/block/pallas_call | solution.py:411
  15.3 0.0 collective-permute-done.low_ref
  15.3 0.8 %collective-permute-done.1.high_ref = f32[72,128]{1,0:T(8,128)S(1)} collective-permute-done((f32[72,128]{1,0:T(8,128)S(1)}, f32[72,128]{1,0:T(8,128)S(1)}, u32[]{:S(2)}, u32[]{:S(2)}) %collective-permute-start.1) | collective-permute-done | bytes 36896 | tf_op jit(solution)/shard_map/ppermute | solution.py:409
  16.1 4.7 %collective-permute-start.2 = (f32[72,128]{1,0:T(8,128)S(1)}, f32[72,128]{1,0:T(8,128)S(1)}, u32[]{:S(2)}, u32[]{:S(2)}) collective-permute-start(f32[72,128]{1,0:T(8,128)S(1)} %zface.1), channel_id=1, source_target_pairs={{1,2},{2,1},{3,4},{4,3},{5,6},{6,5},{7,0},{0,7},{9,10},{10,9},{11,... | collective-permute-start | bytes 110600 | tf_op jit(solution)/shard_map/ppermute | solution.py:430
  20.8 1.9 %all-gather = f32[144,128]{1,0:T(8,128)S(1)} all-gather(f32[72,128]{1,0:T(8,128)S(1)} %zface.1), channel_id=2, replica_groups={{0,1},{2,3},{4,5},{6,7},{8,9},{10,11},{12,13},{14,15},{16,17},{18,19},{..., dimensions={0}, use_global_device_ids=true | all-gather | bytes 110592 | tf_op jit(solution)/shard_map/all_gather | solution.py:431
  22.7 0.8 %collective-permute-done.2.odd_ref = f32[72,128]{1,0:T(8,128)S(1)} collective-permute-done((f32[72,128]{1,0:T(8,128)S(1)}, f32[72,128]{1,0:T(8,128)S(1)}, u32[]{:S(2)}, u32[]{:S(2)}) %collective-permute-start.2) | collective-permute-done | bytes 36896 | tf_op jit(solution)/shard_map/ppermute | solution.py:430
  23.5 0.1 xface.1
  23.6 3.7 %collective-permute-start.3 = (f32[152,128]{1,0:T(8,128)S(1)}, f32[152,128]{1,0:T(8,128)S(1)}, u32[]{:S(2)}, u32[]{:S(2)}) collective-permute-start(f32[152,128]{1,0:T(8,128)S(1)} %get-tuple-element.27), channel_id=1, source_target_pairs={{0,64},{64,128},{128,192},{192,256},{256,320},{320,384},{384,448},... | collective-permute-start | bytes 233480 | tf_op jit(solution)/shard_map/ppermute | solution.py:442
  27.2 2.2 %collective-permute-start.4 = (f32[152,128]{1,0:T(8,128)S(1)}, f32[152,128]{1,0:T(8,128)S(1)}, u32[]{:S(2)}, u32[]{:S(2)}) collective-permute-start(f32[152,128]{1,0:T(8,128)S(1)} %get-tuple-element.28), channel_id=1, source_target_pairs={{64,0},{128,64},{192,128},{256,192},{320,256},{384,320},{448,384},... | collective-permute-start | bytes 233480 | tf_op jit(solution)/shard_map/ppermute | solution.py:443
  29.4 3.6 %inner.1 = (bf16[6,32,64,128]{3,2,1,0:T(8,128)(2,1)}, f32[32,64,128]{2,1,0:T(8,128)S(1)}, f32[32,64,128]{2,1,0:T(8,128)S(1)}, f32[32,64,128]{2,1,0:T(8,128)S(1)}...) custom-call(s32[1]{0:T(128)} %bitcast.parity_ref, f32[32,64,128]{2,1,0:T(8,128)S(1)} %get-tuple-element.23.eps_ref, ...), custom_call_target="tpu_custom_call" | custom-call | flops 24000000 | bytes 6000000 | tf_op jit(solution)/shard_map/inner/pallas_call | solution.py:447
  33.0 0.0 collective-permute-done.3.low_ref
  33.1 2.6 %collective-permute-done.4.high_ref = f32[152,128]{1,0:T(8,128)S(1)} collective-permute-done((f32[152,128]{1,0:T(8,128)S(1)}, f32[152,128]{1,0:T(8,128)S(1)}, u32[]{:S(2)}, u32[]{:S(2)}) %collective-permute-start.4) | collective-permute-done | bytes 77856 | tf_op jit(solution)/shard_map/ppermute | solution.py:443
  35.6 1.5 %outer.1 = bf16[6,32,64,128]{3,2,1,0:T(8,128)(2,1)} custom-call(f32[152,128]{1,0:T(8,128)S(1)} %collective-permute-done.3.low_ref, f32[152,128]{1,0:T(8,128)S(1)} %collective-permute-done.4.high_ref, f32[32,64,128]{2,1,0:T(8,128)S(1)} %get-tuple-element.29.yb_in, f32[32,64,128]{2,1,0:T(8,128)S(1)} %get-tuple-element.30.yd_in, ...), custom_call_target="tpu_custom_call", output_to_operand_aliasing={{}: (7, {})} | custom-call | flops 4000000 | bytes 1000000 | tf_op jit(solution)/shard_map/outer/pallas_call | solution.py:468
  (1 shorter events, 0.0 us)
Async XLA Ops:
  1.6 13.7 %collective-permute-start = (f32[72,128]{1,0:T(8,128)S(1)}, f32[72,128]{1,0:T(8,128)S(1)}, u32[]{:S(2)}, u32[]{:S(2)}) collective-permute-start(f32[72,128]{1,0:T(8,128)S(1)} %get-tuple-element.24), channel_id=1, source_target_pairs={{0,8},{8,16},{16,24},{24,32},{32,40},{40,48},{48,56},{56,0},{1,9},... | collective-permute-start | bytes 110600 | tf_op jit(solution)/shard_map/ppermute | solution.py:408
  5.9 10.2 %collective-permute-start.1 = (f32[72,128]{1,0:T(8,128)S(1)}, f32[72,128]{1,0:T(8,128)S(1)}, u32[]{:S(2)}, u32[]{:S(2)}) collective-permute-start(f32[72,128]{1,0:T(8,128)S(1)} %get-tuple-element.25), channel_id=1, source_target_pairs={{8,0},{16,8},{24,16},{32,24},{40,32},{48,40},{56,48},{0,56},{9,1},... | collective-permute-start | bytes 110600 | tf_op jit(solution)/shard_map/ppermute | solution.py:409
  16.1 7.4 %collective-permute-start.2 = (f32[72,128]{1,0:T(8,128)S(1)}, f32[72,128]{1,0:T(8,128)S(1)}, u32[]{:S(2)}, u32[]{:S(2)}) collective-permute-start(f32[72,128]{1,0:T(8,128)S(1)} %zface.1), channel_id=1, source_target_pairs={{1,2},{2,1},{3,4},{4,3},{5,6},{6,5},{7,0},{0,7},{9,10},{10,9},{11,... | collective-permute-start | bytes 110600 | tf_op jit(solution)/shard_map/ppermute | solution.py:430
  23.6 9.5 %collective-permute-start.3 = (f32[152,128]{1,0:T(8,128)S(1)}, f32[152,128]{1,0:T(8,128)S(1)}, u32[]{:S(2)}, u32[]{:S(2)}) collective-permute-start(f32[152,128]{1,0:T(8,128)S(1)} %get-tuple-element.27), channel_id=1, source_target_pairs={{0,64},{64,128},{128,192},{192,256},{256,320},{320,384},{384,448},... | collective-permute-start | bytes 233480 | tf_op jit(solution)/shard_map/ppermute | solution.py:442
  27.2 8.4 %collective-permute-start.4 = (f32[152,128]{1,0:T(8,128)S(1)}, f32[152,128]{1,0:T(8,128)S(1)}, u32[]{:S(2)}, u32[]{:S(2)}) collective-permute-start(f32[152,128]{1,0:T(8,128)S(1)} %get-tuple-element.28), channel_id=1, source_target_pairs={{64,0},{128,64},{192,128},{256,192},{320,256},{384,320},{448,384},... | collective-permute-start | bytes 233480 | tf_op jit(solution)/shard_map/ppermute | solution.py:443

commit v6 on v5

--- a/solution.py
+++ b/solution.py
@@ -192,7 +192,7 @@
 
 GROUP = 4
 BEHIND = 3 + 4 // GROUP
-EARLY = 3
+EARLY = 4
 
 
 def inner_kernel(

time: 37.4 us -> 37.3 us (level)
  no operation moved by 1% of the time
where the time goes in v6:
time: 37.3 us; the launch traced here: 37 us
  starting transfers between devices  23.4 us (63%)
  Pallas kernels  7.58 us (20%)
  waiting for transfers between devices  4.02 us (11%)
  blocking collectives  1.86 us (5%)
    ppermute x1, starting transfers between devices, local(): y_high = lax.ppermute(y_bwd, 'gy', backward)  8.59 us
    ppermute x1, starting transfers between devices, local(): z_odd = lax.ppermute(z_face, 'gz', odd)  4.74 us
    ppermute x1, starting transfers between devices, local(): y_low = lax.ppermute(y_fwd, 'gy', forward)  4.28 us
    pallas_call x1, Pallas kernels, local(): pl.pallas_call(inner_kernel, in_specs=[SMEM] + [VMEM] * 5, out_specs=[ANY...  3.76 us
    ppermute x1, starting transfers between devices, local(): x_low = lax.ppermute(x_fwd, 'gx', forward)  3.65 us
    ppermute x1, waiting for transfers between devices, local(): x_high = lax.ppermute(x_bwd, 'gx', backward)  2.42 us
    ppermute x1, starting transfers between devices, local(): x_high = lax.ppermute(x_bwd, 'gx', backward)  2.19 us
    all_gather x1, blocking collectives, local(): z_even = lax.all_gather(z_face, 'gz', axis=0, axis_index_groups=pairs)  1.86 us
  transfers between devices with their start and end apart: 5, of which 3 were waited for; matrix products, arithmetic and copies ran while one was open for 0% of the time, Pallas kernels for 12%

profile of v6, /device:TPU:6, one launch (start us, length us, event | category | flops | bytes accessed | tf_op | source)
XLA Modules:
  0.0 37.0 jit_solution(10077917427985678158)
XLA Ops:
  0.0 1.6 %face.1 = (f32[72,128]{1,0:T(8,128)S(1)}, f32[72,128]{1,0:T(8,128)S(1)}, s32[32,64,128]{2,1,0:T(8,128)S(1)}, bf16[32,64,128]{2,1,0:T(8,128)(2,1)S(1)}, f32[8,128]{1,0:T(8,128)S(1)}) custom-call(f32[8]{0:T(128)} %table_hbm.1, s32[32,64,128]{2,1,0:T(8,128)} %mat_hbm.1, bf16[32,64,128]{2,1,0:T(8,128)(2,1)} %gra_hbm.1), custom_call_target="tpu_custom_call" | custom-call | flops 4000000 | bytes 1000000 | tf_op jit(solution)/shard_map/face/pallas_call | solution.py:389
  1.6 4.3 %collective-permute-start = (f32[72,128]{1,0:T(8,128)S(1)}, f32[72,128]{1,0:T(8,128)S(1)}, u32[]{:S(2)}, u32[]{:S(2)}) collective-permute-start(f32[72,128]{1,0:T(8,128)S(1)} %get-tuple-element.24), channel_id=1, source_target_pairs={{0,8},{8,16},{16,24},{24,32},{32,40},{40,48},{48,56},{56,0},{1,9},... | collective-permute-start | bytes 110600 | tf_op jit(solution)/shard_map/ppermute | solution.py:408
  5.9 8.6 %collective-permute-start.1 = (f32[72,128]{1,0:T(8,128)S(1)}, f32[72,128]{1,0:T(8,128)S(1)}, u32[]{:S(2)}, u32[]{:S(2)}) collective-permute-start(f32[72,128]{1,0:T(8,128)S(1)} %get-tuple-element.25), channel_id=1, source_target_pairs={{8,0},{16,8},{24,16},{32,24},{40,32},{48,40},{56,48},{0,56},{9,1},... | collective-permute-start | bytes 110600 | tf_op jit(solution)/shard_map/ppermute | solution.py:409
  14.5 0.8 %block.1 = (f32[32,64,128]{2,1,0:T(8,128)S(1)}, f32[64,128]{1,0:T(8,128)S(1)}) custom-call(f32[8,128]{1,0:T(8,128)S(1)} %get-tuple-element.20.rows_ref, s32[32,64,128]{2,1,0:T(8,128)S(1)} %get-tuple-element.21.mat_ref, bf16[32,64,128]{2,1,0:T(8,128)(2,1)S(1)} %get-tuple-element.22.gra_ref), custom_call_target="tpu_custom_call" | custom-call | flops 12000000 | bytes 3000000 | tf_op jit(solution)/shard_map/block/pallas_call | solution.py:411
  15.3 0.0 collective-permute-done.low_ref
  15.3 0.8 %collective-permute-done.1.high_ref = f32[72,128]{1,0:T(8,128)S(1)} collective-permute-done((f32[72,128]{1,0:T(8,128)S(1)}, f32[72,128]{1,0:T(8,128)S(1)}, u32[]{:S(2)}, u32[]{:S(2)}) %collective-permute-start.1) | collective-permute-done | bytes 36896 | tf_op jit(solution)/shard_map/ppermute | solution.py:409
  16.1 4.7 %collective-permute-start.2 = (f32[72,128]{1,0:T(8,128)S(1)}, f32[72,128]{1,0:T(8,128)S(1)}, u32[]{:S(2)}, u32[]{:S(2)}) collective-permute-start(f32[72,128]{1,0:T(8,128)S(1)} %zface.1), channel_id=1, source_target_pairs={{1,2},{2,1},{3,4},{4,3},{5,6},{6,5},{7,0},{0,7},{9,10},{10,9},{11,... | collective-permute-start | bytes 110600 | tf_op jit(solution)/shard_map/ppermute | solution.py:430
  20.8 1.9 %all-gather = f32[144,128]{1,0:T(8,128)S(1)} all-gather(f32[72,128]{1,0:T(8,128)S(1)} %zface.1), channel_id=2, replica_groups={{0,1},{2,3},{4,5},{6,7},{8,9},{10,11},{12,13},{14,15},{16,17},{18,19},{..., dimensions={0}, use_global_device_ids=true | all-gather | bytes 110592 | tf_op jit(solution)/shard_map/all_gather | solution.py:431
  22.7 0.8 %collective-permute-done.2.odd_ref = f32[72,128]{1,0:T(8,128)S(1)} collective-permute-done((f32[72,128]{1,0:T(8,128)S(1)}, f32[72,128]{1,0:T(8,128)S(1)}, u32[]{:S(2)}, u32[]{:S(2)}) %collective-permute-start.2) | collective-permute-done | bytes 36896 | tf_op jit(solution)/shard_map/ppermute | solution.py:430
  23.5 0.1 xface.1
  23.6 3.7 %collective-permute-start.3 = (f32[152,128]{1,0:T(8,128)S(1)}, f32[152,128]{1,0:T(8,128)S(1)}, u32[]{:S(2)}, u32[]{:S(2)}) collective-permute-start(f32[152,128]{1,0:T(8,128)S(1)} %get-tuple-element.27), channel_id=1, source_target_pairs={{0,64},{64,128},{128,192},{192,256},{256,320},{320,384},{384,448},... | collective-permute-start | bytes 233480 | tf_op jit(solution)/shard_map/ppermute | solution.py:442
  27.2 2.2 %collective-permute-start.4 = (f32[152,128]{1,0:T(8,128)S(1)}, f32[152,128]{1,0:T(8,128)S(1)}, u32[]{:S(2)}, u32[]{:S(2)}) collective-permute-start(f32[152,128]{1,0:T(8,128)S(1)} %get-tuple-element.28), channel_id=1, source_target_pairs={{64,0},{128,64},{192,128},{256,192},{320,256},{384,320},{448,384},... | collective-permute-start | bytes 233480 | tf_op jit(solution)/shard_map/ppermute | solution.py:443
  29.4 3.8 %inner.1 = (bf16[6,32,64,128]{3,2,1,0:T(8,128)(2,1)}, f32[32,64,128]{2,1,0:T(8,128)S(1)}, f32[32,64,128]{2,1,0:T(8,128)S(1)}, f32[32,64,128]{2,1,0:T(8,128)S(1)}...) custom-call(s32[1]{0:T(128)} %bitcast.parity_ref, f32[32,64,128]{2,1,0:T(8,128)S(1)} %get-tuple-element.23.eps_ref, ...), custom_call_target="tpu_custom_call" | custom-call | flops 24000000 | bytes 6000000 | tf_op jit(solution)/shard_map/inner/pallas_call | solution.py:447
  33.2 0.0 collective-permute-done.3.low_ref
  33.2 2.4 %collective-permute-done.4.high_ref = f32[152,128]{1,0:T(8,128)S(1)} collective-permute-done((f32[152,128]{1,0:T(8,128)S(1)}, f32[152,128]{1,0:T(8,128)S(1)}, u32[]{:S(2)}, u32[]{:S(2)}) %collective-permute-start.4) | collective-permute-done | bytes 77856 | tf_op jit(solution)/shard_map/ppermute | solution.py:443
  35.6 1.4 %outer.1 = bf16[6,32,64,128]{3,2,1,0:T(8,128)(2,1)} custom-call(f32[152,128]{1,0:T(8,128)S(1)} %collective-permute-done.3.low_ref, f32[152,128]{1,0:T(8,128)S(1)} %collective-permute-done.4.high_ref, f32[32,64,128]{2,1,0:T(8,128)S(1)} %get-tuple-element.29.yb_in, f32[32,64,128]{2,1,0:T(8,128)S(1)} %get-tuple-element.30.yd_in, ...), custom_call_target="tpu_custom_call", output_to_operand_aliasing={{}: (7, {})} | custom-call | flops 4000000 | bytes 1000000 | tf_op jit(solution)/shard_map/outer/pallas_call | solution.py:468
  (1 shorter events, 0.0 us)
Async XLA Ops:
  1.6 13.7 %collective-permute-start = (f32[72,128]{1,0:T(8,128)S(1)}, f32[72,128]{1,0:T(8,128)S(1)}, u32[]{:S(2)}, u32[]{:S(2)}) collective-permute-start(f32[72,128]{1,0:T(8,128)S(1)} %get-tuple-element.24), channel_id=1, source_target_pairs={{0,8},{8,16},{16,24},{24,32},{32,40},{40,48},{48,56},{56,0},{1,9},... | collective-permute-start | bytes 110600 | tf_op jit(solution)/shard_map/ppermute | solution.py:408
  5.9 10.2 %collective-permute-start.1 = (f32[72,128]{1,0:T(8,128)S(1)}, f32[72,128]{1,0:T(8,128)S(1)}, u32[]{:S(2)}, u32[]{:S(2)}) collective-permute-start(f32[72,128]{1,0:T(8,128)S(1)} %get-tuple-element.25), channel_id=1, source_target_pairs={{8,0},{16,8},{24,16},{32,24},{40,32},{48,40},{56,48},{0,56},{9,1},... | collective-permute-start | bytes 110600 | tf_op jit(solution)/shard_map/ppermute | solution.py:409
  16.1 7.4 %collective-permute-start.2 = (f32[72,128]{1,0:T(8,128)S(1)}, f32[72,128]{1,0:T(8,128)S(1)}, u32[]{:S(2)}, u32[]{:S(2)}) collective-permute-start(f32[72,128]{1,0:T(8,128)S(1)} %zface.1), channel_id=1, source_target_pairs={{1,2},{2,1},{3,4},{4,3},{5,6},{6,5},{7,0},{0,7},{9,10},{10,9},{11,... | collective-permute-start | bytes 110600 | tf_op jit(solution)/shard_map/ppermute | solution.py:430
  23.6 9.6 %collective-permute-start.3 = (f32[152,128]{1,0:T(8,128)S(1)}, f32[152,128]{1,0:T(8,128)S(1)}, u32[]{:S(2)}, u32[]{:S(2)}) collective-permute-start(f32[152,128]{1,0:T(8,128)S(1)} %get-tuple-element.27), channel_id=1, source_target_pairs={{0,64},{64,128},{128,192},{192,256},{256,320},{320,384},{384,448},... | collective-permute-start | bytes 233480 | tf_op jit(solution)/shard_map/ppermute | solution.py:442
  27.2 8.4 %collective-permute-start.4 = (f32[152,128]{1,0:T(8,128)S(1)}, f32[152,128]{1,0:T(8,128)S(1)}, u32[]{:S(2)}, u32[]{:S(2)}) collective-permute-start(f32[152,128]{1,0:T(8,128)S(1)} %get-tuple-element.28), channel_id=1, source_target_pairs={{64,0},{128,64},{192,128},{256,192},{320,256},{384,320},{448,384},... | collective-permute-start | bytes 233480 | tf_op jit(solution)/shard_map/ppermute | solution.py:443

commit v7 on v5

--- a/solution.py
+++ b/solution.py
@@ -74,7 +74,7 @@
     finish_face(fwd_ref, packed[1][6:8], nx)
 
 
-STEP = 8
+STEP = 4
 
 
 def block_kernel(rows_ref, mat_ref, gra_ref, eps_ref, packed_ref):

time: 37.4 us -> 37.6 us (level)
  Pallas kernels: 7.55 us -> 8.11 us
  transfers between devices with their start and end apart: 5 -> 5, of which waited for: 3 -> 3; matrix products, arithmetic and copies ran while one was open for 0% -> 0% of each run, Pallas kernels for 12% -> 13%
where the time goes in v7:
time: 37.6 us; the launch traced here: 37.4 us
  starting transfers between devices  23.5 us (62%)
  Pallas kernels  8.11 us (22%)
  waiting for transfers between devices  3.8 us (10%)
  blocking collectives  1.86 us (5%)
    ppermute x1, starting transfers between devices, local(): y_high = lax.ppermute(y_bwd, 'gy', backward)  8.59 us
    ppermute x1, starting transfers between devices, local(): z_odd = lax.ppermute(z_face, 'gz', odd)  4.82 us
    ppermute x1, starting transfers between devices, local(): y_low = lax.ppermute(y_fwd, 'gy', forward)  4.28 us
    ppermute x1, starting transfers between devices, local(): x_low = lax.ppermute(x_fwd, 'gx', forward)  3.65 us
    pallas_call x1, Pallas kernels, local(): pl.pallas_call(inner_kernel, in_specs=[SMEM] + [VMEM] * 5, out_specs=[ANY...  3.61 us
    ppermute x1, waiting for transfers between devices, local(): x_high = lax.ppermute(x_bwd, 'gx', backward)  2.58 us
    ppermute x1, starting transfers between devices, local(): x_high = lax.ppermute(x_bwd, 'gx', backward)  2.19 us
    all_gather x1, blocking collectives, local(): z_even = lax.all_gather(z_face, 'gz', axis=0, axis_index_groups=pairs)  1.86 us
  transfers between devices with their start and end apart: 5, of which 3 were waited for; matrix products, arithmetic and copies ran while one was open for 0% of the time, Pallas kernels for 13%

profile of v7, /device:TPU:6, one launch (start us, length us, event | category | flops | bytes accessed | tf_op | source)
XLA Modules:
  0.0 37.4 jit_solution(8923976044939479956)
XLA Ops:
  0.0 1.8 %face.1 = (f32[72,128]{1,0:T(8,128)S(1)}, f32[72,128]{1,0:T(8,128)S(1)}, s32[32,64,128]{2,1,0:T(8,128)S(1)}, bf16[32,64,128]{2,1,0:T(8,128)(2,1)S(1)}, f32[8,128]{1,0:T(8,128)S(1)}) custom-call(f32[8]{0:T(128)} %table_hbm.1, s32[32,64,128]{2,1,0:T(8,128)} %mat_hbm.1, bf16[32,64,128]{2,1,0:T(8,128)(2,1)} %gra_hbm.1), custom_call_target="tpu_custom_call" | custom-call | flops 4000000 | bytes 1000000 | tf_op jit(solution)/shard_map/face/pallas_call | solution.py:389
  1.8 4.3 %collective-permute-start = (f32[72,128]{1,0:T(8,128)S(1)}, f32[72,128]{1,0:T(8,128)S(1)}, u32[]{:S(2)}, u32[]{:S(2)}) collective-permute-start(f32[72,128]{1,0:T(8,128)S(1)} %get-tuple-element.24), channel_id=1, source_target_pairs={{0,8},{8,16},{16,24},{24,32},{32,40},{40,48},{48,56},{56,0},{1,9},... | collective-permute-start | bytes 110600 | tf_op jit(solution)/shard_map/ppermute | solution.py:408
  6.1 8.6 %collective-permute-start.1 = (f32[72,128]{1,0:T(8,128)S(1)}, f32[72,128]{1,0:T(8,128)S(1)}, u32[]{:S(2)}, u32[]{:S(2)}) collective-permute-start(f32[72,128]{1,0:T(8,128)S(1)} %get-tuple-element.25), channel_id=1, source_target_pairs={{8,0},{16,8},{24,16},{32,24},{40,32},{48,40},{56,48},{0,56},{9,1},... | collective-permute-start | bytes 110600 | tf_op jit(solution)/shard_map/ppermute | solution.py:409
  14.7 1.1 %block.1 = (f32[32,64,128]{2,1,0:T(8,128)S(1)}, f32[64,128]{1,0:T(8,128)S(1)}) custom-call(f32[8,128]{1,0:T(8,128)S(1)} %get-tuple-element.20.rows_ref, s32[32,64,128]{2,1,0:T(8,128)S(1)} %get-tuple-element.21.mat_ref, bf16[32,64,128]{2,1,0:T(8,128)(2,1)S(1)} %get-tuple-element.22.gra_ref), custom_call_target="tpu_custom_call" | custom-call | flops 12000000 | bytes 3000000 | tf_op jit(solution)/shard_map/block/pallas_call | solution.py:411
  15.8 0.0 collective-permute-done.low_ref
  15.8 0.5 %collective-permute-done.1.high_ref = f32[72,128]{1,0:T(8,128)S(1)} collective-permute-done((f32[72,128]{1,0:T(8,128)S(1)}, f32[72,128]{1,0:T(8,128)S(1)}, u32[]{:S(2)}, u32[]{:S(2)}) %collective-permute-start.1) | collective-permute-done | bytes 36896 | tf_op jit(solution)/shard_map/ppermute | solution.py:409
  16.4 4.8 %collective-permute-start.2 = (f32[72,128]{1,0:T(8,128)S(1)}, f32[72,128]{1,0:T(8,128)S(1)}, u32[]{:S(2)}, u32[]{:S(2)}) collective-permute-start(f32[72,128]{1,0:T(8,128)S(1)} %zface.1), channel_id=1, source_target_pairs={{1,2},{2,1},{3,4},{4,3},{5,6},{6,5},{7,0},{0,7},{9,10},{10,9},{11,... | collective-permute-start | bytes 110600 | tf_op jit(solution)/shard_map/ppermute | solution.py:430
  21.2 1.9 %all-gather = f32[144,128]{1,0:T(8,128)S(1)} all-gather(f32[72,128]{1,0:T(8,128)S(1)} %zface.1), channel_id=2, replica_groups={{0,1},{2,3},{4,5},{6,7},{8,9},{10,11},{12,13},{14,15},{16,17},{18,19},{..., dimensions={0}, use_global_device_ids=true | all-gather | bytes 110592 | tf_op jit(solution)/shard_map/all_gather | solution.py:431
  23.0 0.7 %collective-permute-done.2.odd_ref = f32[72,128]{1,0:T(8,128)S(1)} collective-permute-done((f32[72,128]{1,0:T(8,128)S(1)}, f32[72,128]{1,0:T(8,128)S(1)}, u32[]{:S(2)}, u32[]{:S(2)}) %collective-permute-start.2) | collective-permute-done | bytes 36896 | tf_op jit(solution)/shard_map/ppermute | solution.py:430
  23.8 0.1 xface.1
  23.8 3.7 %collective-permute-start.3 = (f32[152,128]{1,0:T(8,128)S(1)}, f32[152,128]{1,0:T(8,128)S(1)}, u32[]{:S(2)}, u32[]{:S(2)}) collective-permute-start(f32[152,128]{1,0:T(8,128)S(1)} %get-tuple-element.27), channel_id=1, source_target_pairs={{0,64},{64,128},{128,192},{192,256},{256,320},{320,384},{384,448},... | collective-permute-start | bytes 233480 | tf_op jit(solution)/shard_map/ppermute | solution.py:442
  27.5 2.2 %collective-permute-start.4 = (f32[152,128]{1,0:T(8,128)S(1)}, f32[152,128]{1,0:T(8,128)S(1)}, u32[]{:S(2)}, u32[]{:S(2)}) collective-permute-start(f32[152,128]{1,0:T(8,128)S(1)} %get-tuple-element.28), channel_id=1, source_target_pairs={{64,0},{128,64},{192,128},{256,192},{320,256},{384,320},{448,384},... | collective-permute-start | bytes 233480 | tf_op jit(solution)/shard_map/ppermute | solution.py:443
  29.7 3.6 %inner.1 = (bf16[6,32,64,128]{3,2,1,0:T(8,128)(2,1)}, f32[32,64,128]{2,1,0:T(8,128)S(1)}, f32[32,64,128]{2,1,0:T(8,128)S(1)}, f32[32,64,128]{2,1,0:T(8,128)S(1)}...) custom-call(s32[1]{0:T(128)} %bitcast.parity_ref, f32[32,64,128]{2,1,0:T(8,128)S(1)} %get-tuple-element.23.eps_ref, ...), custom_call_target="tpu_custom_call" | custom-call | flops 24000000 | bytes 6000000 | tf_op jit(solution)/shard_map/inner/pallas_call | solution.py:447
  33.3 0.0 collective-permute-done.3.low_ref
  33.3 2.6 %collective-permute-done.4.high_ref = f32[152,128]{1,0:T(8,128)S(1)} collective-permute-done((f32[152,128]{1,0:T(8,128)S(1)}, f32[152,128]{1,0:T(8,128)S(1)}, u32[]{:S(2)}, u32[]{:S(2)}) %collective-permute-start.4) | collective-permute-done | bytes 77856 | tf_op jit(solution)/shard_map/ppermute | solution.py:443
  35.9 1.5 %outer.1 = bf16[6,32,64,128]{3,2,1,0:T(8,128)(2,1)} custom-call(f32[152,128]{1,0:T(8,128)S(1)} %collective-permute-done.3.low_ref, f32[152,128]{1,0:T(8,128)S(1)} %collective-permute-done.4.high_ref, f32[32,64,128]{2,1,0:T(8,128)S(1)} %get-tuple-element.29.yb_in, f32[32,64,128]{2,1,0:T(8,128)S(1)} %get-tuple-element.30.yd_in, ...), custom_call_target="tpu_custom_call", output_to_operand_aliasing={{}: (7, {})} | custom-call | flops 4000000 | bytes 1000000 | tf_op jit(solution)/shard_map/outer/pallas_call | solution.py:468
  (1 shorter events, 0.0 us)
Async XLA Ops:
  1.8 14.0 %collective-permute-start = (f32[72,128]{1,0:T(8,128)S(1)}, f32[72,128]{1,0:T(8,128)S(1)}, u32[]{:S(2)}, u32[]{:S(2)}) collective-permute-start(f32[72,128]{1,0:T(8,128)S(1)} %get-tuple-element.24), channel_id=1, source_target_pairs={{0,8},{8,16},{16,24},{24,32},{32,40},{40,48},{48,56},{56,0},{1,9},... | collective-permute-start | bytes 110600 | tf_op jit(solution)/shard_map/ppermute | solution.py:408
  6.1 10.2 %collective-permute-start.1 = (f32[72,128]{1,0:T(8,128)S(1)}, f32[72,128]{1,0:T(8,128)S(1)}, u32[]{:S(2)}, u32[]{:S(2)}) collective-permute-start(f32[72,128]{1,0:T(8,128)S(1)} %get-tuple-element.25), channel_id=1, source_target_pairs={{8,0},{16,8},{24,16},{32,24},{40,32},{48,40},{56,48},{0,56},{9,1},... | collective-permute-start | bytes 110600 | tf_op jit(solution)/shard_map/ppermute | solution.py:409
  16.4 7.4 %collective-permute-start.2 = (f32[72,128]{1,0:T(8,128)S(1)}, f32[72,128]{1,0:T(8,128)S(1)}, u32[]{:S(2)}, u32[]{:S(2)}) collective-permute-start(f32[72,128]{1,0:T(8,128)S(1)} %zface.1), channel_id=1, source_target_pairs={{1,2},{2,1},{3,4},{4,3},{5,6},{6,5},{7,0},{0,7},{9,10},{10,9},{11,... | collective-permute-start | bytes 110600 | tf_op jit(solution)/shard_map/ppermute | solution.py:430
  23.8 9.5 %collective-permute-start.3 = (f32[152,128]{1,0:T(8,128)S(1)}, f32[152,128]{1,0:T(8,128)S(1)}, u32[]{:S(2)}, u32[]{:S(2)}) collective-permute-start(f32[152,128]{1,0:T(8,128)S(1)} %get-tuple-element.27), channel_id=1, source_target_pairs={{0,64},{64,128},{128,192},{192,256},{256,320},{320,384},{384,448},... | collective-permute-start | bytes 233480 | tf_op jit(solution)/shard_map/ppermute | solution.py:442
  27.5 8.4 %collective-permute-start.4 = (f32[152,128]{1,0:T(8,128)S(1)}, f32[152,128]{1,0:T(8,128)S(1)}, u32[]{:S(2)}, u32[]{:S(2)}) collective-permute-start(f32[152,128]{1,0:T(8,128)S(1)} %get-tuple-element.28), channel_id=1, source_target_pairs={{64,0},{128,64},{192,128},{256,192},{320,256},{384,320},{448,384},... | collective-permute-start | bytes 233480 | tf_op jit(solution)/shard_map/ppermute | solution.py:443
